TPU v7x, 32 devices: a whole 2x2x4 slice. The times are simulated.
32 devices in a mesh: dp: 2 (over x), tp: 4 (over z), pp: 4 (over y, core).
Axes of the slice: x: 2, y: 2, z: 4, core: 2. Of those that a mesh axis runs over, the one named last changes fastest.
Arguments:
- tokens_in: bfloat16 [24, 128, 1024], P('dp'), parts along dimension 0
- targets: bfloat16 [24, 128, 1024], P('dp'), parts along dimension 0
- w_in: bfloat16 [4, 2, 1024, 4096], P('pp', None, None, 'tp')
- w_out: bfloat16 [4, 2, 4096, 1024], P('pp', None, 'tp')
Outputs:
- output 1: float32 [8, 2, 1024, 4096], P(('dp', 'pp'), None, None, 'tp'), parts along dimension 0
- output 2: float32 [8, 2, 4096, 1024], P(('dp', 'pp'), None, 'tp'), parts along dimension 0
- output 3: float32 [2], P('dp'), parts along dimension 0
There are 2 independent parts. A program takes and returns all parts, laid end to end along the dimension named above; an argument that names none is the same for every part.
All inputs are finite; a program needn't handle non-finite values.
Results may differ from a plain program's by a relative error of at most 0.00808713.
Values are sent between devices in bfloat16 or wider.
A program may use at most 1 GiB of HBM per device.

v0:
```python
import jax
import jax.numpy as jnp
from jax import lax
from jax.sharding import PartitionSpec as P


def gelu_back(pre_act, back_grad):
    gelu_pull = jax.vjp(jax.nn.gelu, pre_act.astype(jnp.float32))[1]
    return gelu_pull(back_grad)[0].astype(jnp.bfloat16)


def solution(mesh):
    n_stage = mesh.shape["pp"]
    fwd_pairs = [(src_idx, src_idx + 1) for src_idx in range(n_stage - 1)]
    bwd_pairs = [(src_idx + 1, src_idx) for src_idx in range(n_stage - 1)]

    def device_program(x_loc, y_loc, w_in, w_out):
        n_micro, n_tok, d_model = x_loc.shape
        hidden = w_in.shape[3]
        first_w = [w_in[0, layer_idx] for layer_idx in range(2)]
        second_w = [w_out[0, layer_idx] for layer_idx in range(2)]
        stage_idx = lax.axis_index("pp")
        is_first = stage_idx == 0
        is_last = stage_idx == n_stage - 1
        n_slots = min(n_micro, 2 * n_stage - 1)
        n_ticks = n_micro + 2 * n_stage - 2
        inv_count = 1.0 / (n_micro * n_tok * d_model)
        zero_act = jnp.zeros((n_tok, d_model), jnp.bfloat16)

        def run_tick(tick_idx, loop_state):
            recv_act, recv_grad, store_in, store_pre, store_post, acc_first, acc_second, loss_sum = loop_state
            store_in = list(store_in)
            store_pre = list(store_pre)
            store_post = list(store_post)
            acc_first = list(acc_first)
            acc_second = list(acc_second)
            m_fwd = tick_idx - stage_idx
            ok_fwd = (m_fwd >= 0) & (m_fwd < n_micro)
            m_fwd_c = jnp.clip(m_fwd, 0, n_micro - 1)
            slot_fwd = jnp.where(ok_fwd, m_fwd_c % n_slots, n_slots)
            x_first = lax.dynamic_index_in_dim(x_loc, m_fwd_c, 0, keepdims=False)
            cur_act = jnp.where(is_first, x_first, recv_act)
            for layer_idx in range(2):
                pre_act = jnp.einsum("bd,df->bf", cur_act, first_w[layer_idx], preferred_element_type=jnp.float32).astype(jnp.bfloat16)
                post_act = jax.nn.gelu(pre_act.astype(jnp.float32)).astype(jnp.bfloat16)
                part_out = jnp.einsum("bf,fd->bd", post_act, second_w[layer_idx], preferred_element_type=jnp.float32).astype(jnp.bfloat16)
                branch = lax.psum(part_out, "tp")
                store_in[layer_idx] = lax.dynamic_update_index_in_dim(store_in[layer_idx], cur_act, slot_fwd, 0)
                store_pre[layer_idx] = lax.dynamic_update_index_in_dim(store_pre[layer_idx], pre_act, slot_fwd, 0)
                store_post[layer_idx] = lax.dynamic_update_index_in_dim(store_post[layer_idx], post_act, slot_fwd, 0)
                cur_act = (cur_act.astype(jnp.float32) + branch.astype(jnp.float32)).astype(jnp.bfloat16)
            y_mb = lax.dynamic_index_in_dim(y_loc, m_fwd_c, 0, keepdims=False)
            error_val = cur_act.astype(jnp.float32) - y_mb.astype(jnp.float32)
            loss_sum = loss_sum + jnp.where(is_last & ok_fwd, 0.5 * jnp.sum(error_val * error_val), 0.0)
            m_bwd = tick_idx - (2 * n_stage - 2 - stage_idx)
            ok_bwd = (m_bwd >= 0) & (m_bwd < n_micro)
            slot_bwd = jnp.clip(m_bwd, 0, n_micro - 1) % n_slots
            cur_grad = jnp.where(is_last, (error_val * inv_count).astype(jnp.bfloat16), recv_grad)
            cur_grad = jnp.where(ok_bwd, cur_grad, zero_act)
            for layer_idx in (1, 0):
                act_sv = lax.dynamic_index_in_dim(store_in[layer_idx], slot_bwd, 0, keepdims=False)
                pre_sv = lax.dynamic_index_in_dim(store_pre[layer_idx], slot_bwd, 0, keepdims=False)
                post_sv = lax.dynamic_index_in_dim(store_post[layer_idx], slot_bwd, 0, keepdims=False)
                back_grad = jnp.einsum("bd,fd->bf", cur_grad, second_w[layer_idx], preferred_element_type=jnp.float32)
                gate_grad = gelu_back(pre_sv, back_grad)
                part_in = jnp.einsum("bf,df->bd", gate_grad, first_w[layer_idx], preferred_element_type=jnp.float32).astype(jnp.bfloat16)
                spread = lax.psum(part_in, "tp")
                acc_first[layer_idx] = acc_first[layer_idx] + jnp.einsum("bd,bf->df", act_sv, gate_grad, preferred_element_type=jnp.float32)
                acc_second[layer_idx] = acc_second[layer_idx] + jnp.einsum("bf,bd->fd", post_sv, cur_grad, preferred_element_type=jnp.float32)
                cur_grad = (cur_grad.astype(jnp.float32) + spread.astype(jnp.float32)).astype(jnp.bfloat16)
            recv_act = lax.ppermute(cur_act, "pp", fwd_pairs)
            recv_grad = lax.ppermute(cur_grad, "pp", bwd_pairs)
            return (recv_act, recv_grad, tuple(store_in), tuple(store_pre), tuple(store_post), tuple(acc_first), tuple(acc_second), loss_sum)

        buf_in = jnp.zeros((n_slots + 1, n_tok, d_model), jnp.bfloat16)
        buf_hidden = jnp.zeros((n_slots + 1, n_tok, hidden), jnp.bfloat16)
        zero_first = jnp.zeros((d_model, hidden), jnp.float32)
        zero_second = jnp.zeros((hidden, d_model), jnp.float32)
        init_state = (zero_act, zero_act, (buf_in, buf_in), (buf_hidden, buf_hidden), (buf_hidden, buf_hidden), (zero_first, zero_first), (zero_second, zero_second), jnp.zeros((), jnp.float32))
        final_state = lax.fori_loop(0, n_ticks, run_tick, init_state)
        grad_first = jnp.stack(final_state[5])[None]
        grad_second = jnp.stack(final_state[6])[None]
        loss_val = (lax.psum(final_state[7], "pp") * inv_count).reshape(1)
        return grad_first, grad_second, loss_val

    return jax.shard_map(
        device_program,
        mesh=mesh,
        in_specs=(P("dp", None, None), P("dp", None, None), P("pp", None, None, "tp"), P("pp", None, "tp", None)),
        out_specs=(P(("dp", "pp"), None, None, "tp"), P(("dp", "pp"), None, "tp", None), P("dp")),
        check_vma=False,
    )
```

profile of v0, /device:TPU:0, one launch (start us, length us, event | category | flops | bytes accessed | tf_op | source)
XLA Modules:
  0.0 3151.9 jit_solution(1888574550875729110)
XLA Ops:
  23.3 3095.7 %while.41 = (s32[]{:T(128)}, bf16[128,1024]{1,0:T(8,128)(2,1)}, bf16[128,1024]{1,0:T(8,128)(2,1)S(1)}, bf16[8,128,1024]{2,1,0:T(8,128)(2,1)}, bf16[8,128,1024]{2...) while((s32[]{:T(128)}, bf16[128,1024]{1,0:T(8,128)(2,1)}, ...), condition=%wide.region_6.7_spmd.clone, body=%wide.region_0.6_spmd.clone.sunk | while | flops 3250323456 | bytes 109317208 | solution.py:80
  27.8 38.4 %all-reduce.5.cloned.1.call-done = bf16[128,1024]{1,0:T(8,128)(2,1)} async-done(((bf16[128,1024]{1,0:T(8,128)(2,1)}), bf16[128,1024]{1,0:T(8,128)(2,1)}) %all-reduce.5.cloned.1.call-update) | async-done | bytes 262160 | tf_op jit(solution)/shard_map/while/body/eval_jaxpr/psum | solution.py:47
  71.5 34.5 %all-reduce.7.cloned.1.call-done = bf16[128,1024]{1,0:T(8,128)(2,1)} async-done(((bf16[128,1024]{1,0:T(8,128)(2,1)}), bf16[128,1024]{1,0:T(8,128)(2,1)}) %all-reduce.7.cloned.1.call-update) | async-done | bytes 262160 | tf_op jit(solution)/shard_map/while/body/eval_jaxpr/psum | solution.py:47
  200.6 36.6 %all-reduce.5.cloned.1.call-done = bf16[128,1024]{1,0:T(8,128)(2,1)} async-done(((bf16[128,1024]{1,0:T(8,128)(2,1)}), bf16[128,1024]{1,0:T(8,128)(2,1)}) %all-reduce.5.cloned.1.call-update) | async-done | bytes 262160 | tf_op jit(solution)/shard_map/while/body/eval_jaxpr/psum | solution.py:47
  242.5 34.5 %all-reduce.7.cloned.1.call-done = bf16[128,1024]{1,0:T(8,128)(2,1)} async-done(((bf16[128,1024]{1,0:T(8,128)(2,1)}), bf16[128,1024]{1,0:T(8,128)(2,1)}) %all-reduce.7.cloned.1.call-update) | async-done | bytes 262160 | tf_op jit(solution)/shard_map/while/body/eval_jaxpr/psum | solution.py:47
  373.0 36.2 %all-reduce.5.cloned.1.call-done = bf16[128,1024]{1,0:T(8,128)(2,1)} async-done(((bf16[128,1024]{1,0:T(8,128)(2,1)}), bf16[128,1024]{1,0:T(8,128)(2,1)}) %all-reduce.5.cloned.1.call-update) | async-done | bytes 262160 | tf_op jit(solution)/shard_map/while/body/eval_jaxpr/psum | solution.py:47
  545.0 36.2 %all-reduce.5.cloned.1.call-done = bf16[128,1024]{1,0:T(8,128)(2,1)} async-done(((bf16[128,1024]{1,0:T(8,128)(2,1)}), bf16[128,1024]{1,0:T(8,128)(2,1)}) %all-reduce.5.cloned.1.call-update) | async-done | bytes 262160 | tf_op jit(solution)/shard_map/while/body/eval_jaxpr/psum | solution.py:47
  716.9 36.1 %all-reduce.5.cloned.1.call-done = bf16[128,1024]{1,0:T(8,128)(2,1)} async-done(((bf16[128,1024]{1,0:T(8,128)(2,1)}), bf16[128,1024]{1,0:T(8,128)(2,1)}) %all-reduce.5.cloned.1.call-update) | async-done | bytes 262160 | tf_op jit(solution)/shard_map/while/body/eval_jaxpr/psum | solution.py:47
  758.3 34.5 %all-reduce.7.cloned.1.call-done = bf16[128,1024]{1,0:T(8,128)(2,1)} async-done(((bf16[128,1024]{1,0:T(8,128)(2,1)}), bf16[128,1024]{1,0:T(8,128)(2,1)}) %all-reduce.7.cloned.1.call-update) | async-done | bytes 262160 | tf_op jit(solution)/shard_map/while/body/eval_jaxpr/psum | solution.py:47
  888.8 36.2 %all-reduce.5.cloned.1.call-done = bf16[128,1024]{1,0:T(8,128)(2,1)} async-done(((bf16[128,1024]{1,0:T(8,128)(2,1)}), bf16[128,1024]{1,0:T(8,128)(2,1)}) %all-reduce.5.cloned.1.call-update) | async-done | bytes 262160 | tf_op jit(solution)/shard_map/while/body/eval_jaxpr/psum | solution.py:47
  930.3 34.5 %all-reduce.7.cloned.1.call-done = bf16[128,1024]{1,0:T(8,128)(2,1)} async-done(((bf16[128,1024]{1,0:T(8,128)(2,1)}), bf16[128,1024]{1,0:T(8,128)(2,1)}) %all-reduce.7.cloned.1.call-update) | async-done | bytes 262160 | tf_op jit(solution)/shard_map/while/body/eval_jaxpr/psum | solution.py:47
  1060.7 36.2 %all-reduce.5.cloned.1.call-done = bf16[128,1024]{1,0:T(8,128)(2,1)} async-done(((bf16[128,1024]{1,0:T(8,128)(2,1)}), bf16[128,1024]{1,0:T(8,128)(2,1)}) %all-reduce.5.cloned.1.call-update) | async-done | bytes 262160 | tf_op jit(solution)/shard_map/while/body/eval_jaxpr/psum | solution.py:47
  1232.6 36.2 %all-reduce.5.cloned.1.call-done = bf16[128,1024]{1,0:T(8,128)(2,1)} async-done(((bf16[128,1024]{1,0:T(8,128)(2,1)}), bf16[128,1024]{1,0:T(8,128)(2,1)}) %all-reduce.5.cloned.1.call-update) | async-done | bytes 262160 | tf_op jit(solution)/shard_map/while/body/eval_jaxpr/psum | solution.py:47
  1404.5 36.1 %all-reduce.5.cloned.1.call-done = bf16[128,1024]{1,0:T(8,128)(2,1)} async-done(((bf16[128,1024]{1,0:T(8,128)(2,1)}), bf16[128,1024]{1,0:T(8,128)(2,1)}) %all-reduce.5.cloned.1.call-update) | async-done | bytes 262160 | tf_op jit(solution)/shard_map/while/body/eval_jaxpr/psum | solution.py:47
  1576.4 36.1 %all-reduce.5.cloned.1.call-done = bf16[128,1024]{1,0:T(8,128)(2,1)} async-done(((bf16[128,1024]{1,0:T(8,128)(2,1)}), bf16[128,1024]{1,0:T(8,128)(2,1)}) %all-reduce.5.cloned.1.call-update) | async-done | bytes 262160 | tf_op jit(solution)/shard_map/while/body/eval_jaxpr/psum | solution.py:47
  1748.2 36.2 %all-reduce.5.cloned.1.call-done = bf16[128,1024]{1,0:T(8,128)(2,1)} async-done(((bf16[128,1024]{1,0:T(8,128)(2,1)}), bf16[128,1024]{1,0:T(8,128)(2,1)}) %all-reduce.5.cloned.1.call-update) | async-done | bytes 262160 | tf_op jit(solution)/shard_map/while/body/eval_jaxpr/psum | solution.py:47
  1920.2 36.2 %all-reduce.5.cloned.1.call-done = bf16[128,1024]{1,0:T(8,128)(2,1)} async-done(((bf16[128,1024]{1,0:T(8,128)(2,1)}), bf16[128,1024]{1,0:T(8,128)(2,1)}) %all-reduce.5.cloned.1.call-update) | async-done | bytes 262160 | tf_op jit(solution)/shard_map/while/body/eval_jaxpr/psum | solution.py:47
  2092.1 36.1 %all-reduce.5.cloned.1.call-done = bf16[128,1024]{1,0:T(8,128)(2,1)} async-done(((bf16[128,1024]{1,0:T(8,128)(2,1)}), bf16[128,1024]{1,0:T(8,128)(2,1)}) %all-reduce.5.cloned.1.call-update) | async-done | bytes 262160 | tf_op jit(solution)/shard_map/while/body/eval_jaxpr/psum | solution.py:47
  2264.0 36.1 %all-reduce.5.cloned.1.call-done = bf16[128,1024]{1,0:T(8,128)(2,1)} async-done(((bf16[128,1024]{1,0:T(8,128)(2,1)}), bf16[128,1024]{1,0:T(8,128)(2,1)}) %all-reduce.5.cloned.1.call-update) | async-done | bytes 262160 | tf_op jit(solution)/shard_map/while/body/eval_jaxpr/psum | solution.py:47
  2435.9 36.1 %all-reduce.5.cloned.1.call-done = bf16[128,1024]{1,0:T(8,128)(2,1)} async-done(((bf16[128,1024]{1,0:T(8,128)(2,1)}), bf16[128,1024]{1,0:T(8,128)(2,1)}) %all-reduce.5.cloned.1.call-update) | async-done | bytes 262160 | tf_op jit(solution)/shard_map/while/body/eval_jaxpr/psum | solution.py:47
  2607.8 36.2 %all-reduce.5.cloned.1.call-done = bf16[128,1024]{1,0:T(8,128)(2,1)} async-done(((bf16[128,1024]{1,0:T(8,128)(2,1)}), bf16[128,1024]{1,0:T(8,128)(2,1)}) %all-reduce.5.cloned.1.call-update) | async-done | bytes 262160 | tf_op jit(solution)/shard_map/while/body/eval_jaxpr/psum | solution.py:47
  2649.3 34.5 %all-reduce.7.cloned.1.call-done = bf16[128,1024]{1,0:T(8,128)(2,1)} async-done(((bf16[128,1024]{1,0:T(8,128)(2,1)}), bf16[128,1024]{1,0:T(8,128)(2,1)}) %all-reduce.7.cloned.1.call-update) | async-done | bytes 262160 | tf_op jit(solution)/shard_map/while/body/eval_jaxpr/psum | solution.py:47
  2779.8 36.2 %all-reduce.5.cloned.1.call-done = bf16[128,1024]{1,0:T(8,128)(2,1)} async-done(((bf16[128,1024]{1,0:T(8,128)(2,1)}), bf16[128,1024]{1,0:T(8,128)(2,1)}) %all-reduce.5.cloned.1.call-update) | async-done | bytes 262160 | tf_op jit(solution)/shard_map/while/body/eval_jaxpr/psum | solution.py:47
  2951.7 36.2 %all-reduce.5.cloned.1.call-done = bf16[128,1024]{1,0:T(8,128)(2,1)} async-done(((bf16[128,1024]{1,0:T(8,128)(2,1)}), bf16[128,1024]{1,0:T(8,128)(2,1)}) %all-reduce.5.cloned.1.call-update) | async-done | bytes 262160 | tf_op jit(solution)/shard_map/while/body/eval_jaxpr/psum | solution.py:47
  (805 shorter events, 2296.5 us)
Async XLA Ops:
  70.6 79.7 %all-reduce.9.cloned.1.call-start = ((), (), s32[]{:S(2)}) async-start(), calls=%async_computation.2 | async-start | bytes 524288 | tf_op jit(solution)/shard_map/while/body/eval_jaxpr/psum | solution.py:67
  107.9 88.1 %collective-permute-start = (bf16[128,1024]{1,0:T(8,128)(2,1)S(1)}, bf16[128,1024]{1,0:T(8,128)(2,1)}, u32[]{:S(2)}, u32[]{:S(2)}) collective-permute-start(bf16[128,1024]{1,0:T(8,128)(2,1)S(1)} %get-tuple-element.903), channel_id=1, source_target_pairs={{0,1},{1,2},{2,3},{4,5},{5,6},{6,7},{8,9},{9,10},{10,11},{12,13},{... | collective-permute-start | bytes 786440 | tf_op jit(solution)/shard_map/while/body/eval_jaxpr/ppermute | solution.py:71
  241.7 79.7 %all-reduce.9.cloned.1.call-start = ((), (), s32[]{:S(2)}) async-start(), calls=%async_computation.2 | async-start | bytes 524288 | tf_op jit(solution)/shard_map/while/body/eval_jaxpr/psum | solution.py:67
  279.0 89.4 %collective-permute-start = (bf16[128,1024]{1,0:T(8,128)(2,1)S(1)}, bf16[128,1024]{1,0:T(8,128)(2,1)}, u32[]{:S(2)}, u32[]{:S(2)}) collective-permute-start(bf16[128,1024]{1,0:T(8,128)(2,1)S(1)} %get-tuple-element.903), channel_id=1, source_target_pairs={{0,1},{1,2},{2,3},{4,5},{5,6},{6,7},{8,9},{9,10},{10,11},{12,13},{... | collective-permute-start | bytes 786440 | tf_op jit(solution)/shard_map/while/body/eval_jaxpr/ppermute | solution.py:71
  450.9 89.4 %collective-permute-start = (bf16[128,1024]{1,0:T(8,128)(2,1)S(1)}, bf16[128,1024]{1,0:T(8,128)(2,1)}, u32[]{:S(2)}, u32[]{:S(2)}) collective-permute-start(bf16[128,1024]{1,0:T(8,128)(2,1)S(1)} %get-tuple-element.903), channel_id=1, source_target_pairs={{0,1},{1,2},{2,3},{4,5},{5,6},{6,7},{8,9},{9,10},{10,11},{12,13},{... | collective-permute-start | bytes 786440 | tf_op jit(solution)/shard_map/while/body/eval_jaxpr/ppermute | solution.py:71
  585.6 79.7 %all-reduce.9.cloned.1.call-start = ((), (), s32[]{:S(2)}) async-start(), calls=%async_computation.2 | async-start | bytes 524288 | tf_op jit(solution)/shard_map/while/body/eval_jaxpr/psum | solution.py:67
  622.9 89.4 %collective-permute-start = (bf16[128,1024]{1,0:T(8,128)(2,1)S(1)}, bf16[128,1024]{1,0:T(8,128)(2,1)}, u32[]{:S(2)}, u32[]{:S(2)}) collective-permute-start(bf16[128,1024]{1,0:T(8,128)(2,1)S(1)} %get-tuple-element.903), channel_id=1, source_target_pairs={{0,1},{1,2},{2,3},{4,5},{5,6},{6,7},{8,9},{9,10},{10,11},{12,13},{... | collective-permute-start | bytes 786440 | tf_op jit(solution)/shard_map/while/body/eval_jaxpr/ppermute | solution.py:71
  794.8 89.4 %collective-permute-start = (bf16[128,1024]{1,0:T(8,128)(2,1)S(1)}, bf16[128,1024]{1,0:T(8,128)(2,1)}, u32[]{:S(2)}, u32[]{:S(2)}) collective-permute-start(bf16[128,1024]{1,0:T(8,128)(2,1)S(1)} %get-tuple-element.903), channel_id=1, source_target_pairs={{0,1},{1,2},{2,3},{4,5},{5,6},{6,7},{8,9},{9,10},{10,11},{12,13},{... | collective-permute-start | bytes 786440 | tf_op jit(solution)/shard_map/while/body/eval_jaxpr/ppermute | solution.py:71
  966.7 89.4 %collective-permute-start = (bf16[128,1024]{1,0:T(8,128)(2,1)S(1)}, bf16[128,1024]{1,0:T(8,128)(2,1)}, u32[]{:S(2)}, u32[]{:S(2)}) collective-permute-start(bf16[128,1024]{1,0:T(8,128)(2,1)S(1)} %get-tuple-element.903), channel_id=1, source_target_pairs={{0,1},{1,2},{2,3},{4,5},{5,6},{6,7},{8,9},{9,10},{10,11},{12,13},{... | collective-permute-start | bytes 786440 | tf_op jit(solution)/shard_map/while/body/eval_jaxpr/ppermute | solution.py:71
  1138.5 89.4 %collective-permute-start = (bf16[128,1024]{1,0:T(8,128)(2,1)S(1)}, bf16[128,1024]{1,0:T(8,128)(2,1)}, u32[]{:S(2)}, u32[]{:S(2)}) collective-permute-start(bf16[128,1024]{1,0:T(8,128)(2,1)S(1)} %get-tuple-element.903), channel_id=1, source_target_pairs={{0,1},{1,2},{2,3},{4,5},{5,6},{6,7},{8,9},{9,10},{10,11},{12,13},{... | collective-permute-start | bytes 786440 | tf_op jit(solution)/shard_map/while/body/eval_jaxpr/ppermute | solution.py:71
  1310.4 89.4 %collective-permute-start = (bf16[128,1024]{1,0:T(8,128)(2,1)S(1)}, bf16[128,1024]{1,0:T(8,128)(2,1)}, u32[]{:S(2)}, u32[]{:S(2)}) collective-permute-start(bf16[128,1024]{1,0:T(8,128)(2,1)S(1)} %get-tuple-element.903), channel_id=1, source_target_pairs={{0,1},{1,2},{2,3},{4,5},{5,6},{6,7},{8,9},{9,10},{10,11},{12,13},{... | collective-permute-start | bytes 786440 | tf_op jit(solution)/shard_map/while/body/eval_jaxpr/ppermute | solution.py:71
  1445.0 79.7 %all-reduce.9.cloned.1.call-start = ((), (), s32[]{:S(2)}) async-start(), calls=%async_computation.2 | async-start | bytes 524288 | tf_op jit(solution)/shard_map/while/body/eval_jaxpr/psum | solution.py:67
  1482.3 89.4 %collective-permute-start = (bf16[128,1024]{1,0:T(8,128)(2,1)S(1)}, bf16[128,1024]{1,0:T(8,128)(2,1)}, u32[]{:S(2)}, u32[]{:S(2)}) collective-permute-start(bf16[128,1024]{1,0:T(8,128)(2,1)S(1)} %get-tuple-element.903), channel_id=1, source_target_pairs={{0,1},{1,2},{2,3},{4,5},{5,6},{6,7},{8,9},{9,10},{10,11},{12,13},{... | collective-permute-start | bytes 786440 | tf_op jit(solution)/shard_map/while/body/eval_jaxpr/ppermute | solution.py:71
  1654.2 89.4 %collective-permute-start = (bf16[128,1024]{1,0:T(8,128)(2,1)S(1)}, bf16[128,1024]{1,0:T(8,128)(2,1)}, u32[]{:S(2)}, u32[]{:S(2)}) collective-permute-start(bf16[128,1024]{1,0:T(8,128)(2,1)S(1)} %get-tuple-element.903), channel_id=1, source_target_pairs={{0,1},{1,2},{2,3},{4,5},{5,6},{6,7},{8,9},{9,10},{10,11},{12,13},{... | collective-permute-start | bytes 786440 | tf_op jit(solution)/shard_map/while/body/eval_jaxpr/ppermute | solution.py:71
  1826.1 89.4 %collective-permute-start = (bf16[128,1024]{1,0:T(8,128)(2,1)S(1)}, bf16[128,1024]{1,0:T(8,128)(2,1)}, u32[]{:S(2)}, u32[]{:S(2)}) collective-permute-start(bf16[128,1024]{1,0:T(8,128)(2,1)S(1)} %get-tuple-element.903), channel_id=1, source_target_pairs={{0,1},{1,2},{2,3},{4,5},{5,6},{6,7},{8,9},{9,10},{10,11},{12,13},{... | collective-permute-start | bytes 786440 | tf_op jit(solution)/shard_map/while/body/eval_jaxpr/ppermute | solution.py:71
  1960.7 79.7 %all-reduce.9.cloned.1.call-start = ((), (), s32[]{:S(2)}) async-start(), calls=%async_computation.2 | async-start | bytes 524288 | tf_op jit(solution)/shard_map/while/body/eval_jaxpr/psum | solution.py:67
  1998.0 89.4 %collective-permute-start = (bf16[128,1024]{1,0:T(8,128)(2,1)S(1)}, bf16[128,1024]{1,0:T(8,128)(2,1)}, u32[]{:S(2)}, u32[]{:S(2)}) collective-permute-start(bf16[128,1024]{1,0:T(8,128)(2,1)S(1)} %get-tuple-element.903), channel_id=1, source_target_pairs={{0,1},{1,2},{2,3},{4,5},{5,6},{6,7},{8,9},{9,10},{10,11},{12,13},{... | collective-permute-start | bytes 786440 | tf_op jit(solution)/shard_map/while/body/eval_jaxpr/ppermute | solution.py:71
  2169.9 89.4 %collective-permute-start = (bf16[128,1024]{1,0:T(8,128)(2,1)S(1)}, bf16[128,1024]{1,0:T(8,128)(2,1)}, u32[]{:S(2)}, u32[]{:S(2)}) collective-permute-start(bf16[128,1024]{1,0:T(8,128)(2,1)S(1)} %get-tuple-element.903), channel_id=1, source_target_pairs={{0,1},{1,2},{2,3},{4,5},{5,6},{6,7},{8,9},{9,10},{10,11},{12,13},{... | collective-permute-start | bytes 786440 | tf_op jit(solution)/shard_map/while/body/eval_jaxpr/ppermute | solution.py:71
  2341.8 89.4 %collective-permute-start = (bf16[128,1024]{1,0:T(8,128)(2,1)S(1)}, bf16[128,1024]{1,0:T(8,128)(2,1)}, u32[]{:S(2)}, u32[]{:S(2)}) collective-permute-start(bf16[128,1024]{1,0:T(8,128)(2,1)S(1)} %get-tuple-element.903), channel_id=1, source_target_pairs={{0,1},{1,2},{2,3},{4,5},{5,6},{6,7},{8,9},{9,10},{10,11},{12,13},{... | collective-permute-start | bytes 786440 | tf_op jit(solution)/shard_map/while/body/eval_jaxpr/ppermute | solution.py:71
  2476.4 79.7 %all-reduce.9.cloned.1.call-start = ((), (), s32[]{:S(2)}) async-start(), calls=%async_computation.2 | async-start | bytes 524288 | tf_op jit(solution)/shard_map/while/body/eval_jaxpr/psum | solution.py:67
  2513.7 89.4 %collective-permute-start = (bf16[128,1024]{1,0:T(8,128)(2,1)S(1)}, bf16[128,1024]{1,0:T(8,128)(2,1)}, u32[]{:S(2)}, u32[]{:S(2)}) collective-permute-start(bf16[128,1024]{1,0:T(8,128)(2,1)S(1)} %get-tuple-element.903), channel_id=1, source_target_pairs={{0,1},{1,2},{2,3},{4,5},{5,6},{6,7},{8,9},{9,10},{10,11},{12,13},{... | collective-permute-start | bytes 786440 | tf_op jit(solution)/shard_map/while/body/eval_jaxpr/ppermute | solution.py:71
  2685.7 89.4 %collective-permute-start = (bf16[128,1024]{1,0:T(8,128)(2,1)S(1)}, bf16[128,1024]{1,0:T(8,128)(2,1)}, u32[]{:S(2)}, u32[]{:S(2)}) collective-permute-start(bf16[128,1024]{1,0:T(8,128)(2,1)S(1)} %get-tuple-element.903), channel_id=1, source_target_pairs={{0,1},{1,2},{2,3},{4,5},{5,6},{6,7},{8,9},{9,10},{10,11},{12,13},{... | collective-permute-start | bytes 786440 | tf_op jit(solution)/shard_map/while/body/eval_jaxpr/ppermute | solution.py:71
  2857.7 89.4 %collective-permute-start = (bf16[128,1024]{1,0:T(8,128)(2,1)S(1)}, bf16[128,1024]{1,0:T(8,128)(2,1)}, u32[]{:S(2)}, u32[]{:S(2)}) collective-permute-start(bf16[128,1024]{1,0:T(8,128)(2,1)S(1)} %get-tuple-element.903), channel_id=1, source_target_pairs={{0,1},{1,2},{2,3},{4,5},{5,6},{6,7},{8,9},{9,10},{10,11},{12,13},{... | collective-permute-start | bytes 786440 | tf_op jit(solution)/shard_map/while/body/eval_jaxpr/ppermute | solution.py:71
  3029.6 89.4 %collective-permute-start = (bf16[128,1024]{1,0:T(8,128)(2,1)S(1)}, bf16[128,1024]{1,0:T(8,128)(2,1)}, u32[]{:S(2)}, u32[]{:S(2)}) collective-permute-start(bf16[128,1024]{1,0:T(8,128)(2,1)S(1)} %get-tuple-element.903), channel_id=1, source_target_pairs={{0,1},{1,2},{2,3},{4,5},{5,6},{6,7},{8,9},{9,10},{10,11},{12,13},{... | collective-permute-start | bytes 786440 | tf_op jit(solution)/shard_map/while/body/eval_jaxpr/ppermute | solution.py:71
  (193 other events, 4872.7 us)
Sparse Core Ops, SparseCore 0:
  27.9 38.2 all-reduce.4
  200.7 36.4 all-reduce.4
  373.1 36.0 all-reduce.4
  457.8 35.4 all-reduce.8
  545.0 36.0 all-reduce.4
  629.7 35.4 all-reduce.8
  717.0 36.0 all-reduce.4
  888.8 36.0 all-reduce.4
  1060.7 36.0 all-reduce.4
  1232.7 36.0 all-reduce.4
  1404.5 36.0 all-reduce.4
  1489.2 35.4 all-reduce.8
  1576.5 36.0 all-reduce.4
  1748.3 36.0 all-reduce.4
  1920.2 36.0 all-reduce.4
  2092.1 36.0 all-reduce.4
  2176.8 35.4 all-reduce.8
  2264.1 35.9 all-reduce.4
  2348.7 35.4 all-reduce.8
  2436.0 36.0 all-reduce.4
  2520.6 35.4 all-reduce.8
  2607.9 36.0 all-reduce.4
  2779.8 36.0 all-reduce.4
  2951.8 36.0 all-reduce.4
  (48 shorter events, 1689.4 us)
where the time goes:
time: 3160 us; the launch traced here: 3150 us
  waiting for transfers between devices  2270 us (72%)
  matrix products  624 us (20%)
  other arithmetic  137 us (4%)
  starting transfers between devices  64.3 us (2%)
    psum x36, waiting for transfers between devices, run_tick(): branch = lax.psum(part_out, 'tp')  1270 us
    psum x36, waiting for transfers between devices, run_tick(): spread = lax.psum(part_in, 'tp')  996 us
    dot_general x36, matrix products, run_tick(): jnp.einsum('bd,bf->df', act_sv, gate_grad, preferred_element_type=jnp.flo...  182 us
    dot_general x36, matrix products, run_tick(): jnp.einsum('bf,bd->fd', post_sv, cur_grad, preferred_element_type=jnp.flo...  177 us
    dot_general x36, matrix products, run_tick(): jnp.einsum('bd,df->bf', cur_act, first_w[layer_idx], preferred_element_ty...  80.7 us
    dot_general x36, matrix products, run_tick(): jnp.einsum('bf,df->bd', gate_grad, first_w[layer_idx], preferred_element_...  75.6 us
    dot_general x36, matrix products, run_tick(): jnp.einsum('bd,fd->bf', cur_grad, second_w[layer_idx], preferred_element_...  63.3 us
  transfers between devices with their start and end apart: 108, of which 72 were waited for; matrix products, arithmetic and copies ran while one was open for 17% of the time, Pallas kernels for 0%

commit v1 on v0

v1 whole, which is shorter than its diff:
```python
import functools
import math

import jax
import jax.numpy as jnp
from jax import lax
from jax.experimental import pallas as pl
from jax.experimental.pallas import tpu as pltpu
from jax.sharding import PartitionSpec as P

BF = jnp.bfloat16
F32 = jnp.float32
NP = 4
RING = 4
GC = math.sqrt(2.0 / math.pi)
NT = (((1,), (1,)), ((), ()))
MESH = pl.DeviceIdType.MESH


def gelu_f(x):
    return x * (0.5 + 0.5 * jnp.tanh(GC * (x + 0.044715 * (x * x * x))))


def gelu_d(x):
    x2 = x * x
    th = jnp.tanh(GC * (x + 0.044715 * (x * x2)))
    return 0.5 + 0.5 * th + (0.5 * x) * (1.0 - th * th) * (GC + (3 * 0.044715 * GC) * x2)


def step_kernel(n_stage, n_tp, inv_count, x_hbm, t_hbm, w1_hbm, w2_hbm,
                a_out, d_out, g_out, z_out, loss_out,
                w1, w2, act, gbuf, zbuf, pbuf, qbuf, sbuf, obuf, own, tbuf, lacc, ltile,
                xsem, wsem, psem, qsem, ssem, oesem, oosem, ldsem, tsem, outsem, lsend, lrecv):
    n_micro, _, n_tok, dp_cols = act.shape[1:]
    hid = gbuf.shape[3]
    hb = hid // NP
    n_layer = 2 * n_stage
    stage = lax.axis_index("pp")
    z = lax.axis_index("tp")
    is_mid = (z == 1) | (z == 2)
    is_end = jnp.logical_not(is_mid)
    partner = z + 1 - 2 * lax.rem(z, 2)
    other = n_tp - 1 - z
    first = stage == 0
    last = stage == n_stage - 1
    offs = (2 * stage, 2 * stage + 1, 2 * n_layer - 2 - 2 * stage, 2 * n_layer - 1 - 2 * stage)

    def rcopy(src, dst, s_sem, r_sem, tp, pp):
        return pltpu.make_async_remote_copy(src_ref=src, dst_ref=dst, send_sem=s_sem, recv_sem=r_sem,
                                            device_id={"tp": tp, "pp": pp}, device_id_type=MESH)

    def wait_in(ref, sem):
        pltpu.make_async_copy(ref, ref, sem).wait()

    loads = []
    for k in range(2):
        loads.append(pltpu.make_async_copy(w1_hbm.at[0, k], w1.at[k], ldsem.at[k]))
        loads.append(pltpu.make_async_copy(w2_hbm.at[0, k], w2.at[k], ldsem.at[2 + k]))
    for ld in loads:
        ld.start()

    @pl.when(first)
    def _():
        @pl.loop(0, n_micro)
        def _(m):
            for c in range(NP):
                pltpu.make_async_copy(x_hbm.at[m, :, pl.ds(c * dp_cols, dp_cols)], act.at[0, m, c], xsem.at[0, m, c]).start()

    @pl.when(last & is_mid)
    def _():
        @pl.loop(0, n_micro)
        def _(m):
            for c in range(NP):
                pltpu.make_async_copy(t_hbm.at[m, :, pl.ds(c * dp_cols, dp_cols)], tbuf.at[m, c], tsem).start()

    lacc[...] = jnp.zeros_like(lacc)
    for ld in loads:
        ld.wait()

    @pl.when(last & is_mid)
    def _():
        wait_in(tbuf, tsem)

    def emit_piece(slot, m, c, part):
        @pl.when(is_end)
        def _():
            sbuf[slot, c] = part.astype(BF)
            r = lax.rem(m, RING)
            rcopy(sbuf.at[slot, c], pbuf.at[slot, r, c], ssem.at[slot], psem.at[slot, r, c], partner, stage).start()

        @pl.when(is_mid)
        def _():
            own[slot % 2, c] = part

    def load_full(ai, m):
        return jnp.concatenate([act[ai, m, c] for c in range(NP)], axis=1)

    def put_act(src_idx, m, dst, sem):
        for c in range(NP):
            pltpu.make_async_copy(act.at[src_idx, m, c],
                                  dst.at[src_idx % 2, pl.ds(m * n_tok, n_tok), pl.ds(c * dp_cols, dp_cols)], sem).start()

    def do_a(slot, m):
        fwd = slot < 2
        k = slot if fwd else 3 - slot
        ai = k if fwd else 2 + k
        r = lax.rem(m, RING)
        if slot == 0:
            for c in range(NP):
                wait_in(act.at[ai, m, c], xsem.at[0, m, c])
        elif slot == 2:
            @pl.when(jnp.logical_not(last & is_mid))
            def _():
                for c in range(NP):
                    wait_in(act.at[ai, m, c], xsem.at[1, m, c])
        else:
            @pl.when(is_end)
            def _():
                for c in range(NP):
                    wait_in(act.at[ai, m, c], wsem.at[0 if fwd else 1, r, c])

        @pl.when(is_end & (m > 0) & (jnp.logical_not(first) if slot == 3 else True))
        def _():
            wait_in(sbuf.at[slot], ssem.at[slot])

        put_act(ai, m, a_out if fwd else d_out, outsem.at[0 if fwd else 1])
        rows = pl.ds(m * n_tok, n_tok)
        if fwd:
            a = load_full(ai, m)
            for n in range(NP):
                cs = pl.ds(n * hb, hb)
                u = jnp.dot(a, w1[k, :, cs], preferred_element_type=F32).astype(BF)
                gbuf[k, m, :, cs] = u
                zbuf[k, m, :, cs] = gelu_f(u.astype(F32)).astype(BF)
            pltpu.make_async_copy(zbuf.at[k, m], z_out.at[k, rows], outsem.at[2]).start()
            zz = zbuf[k, m]
            for c in range(NP):
                emit_piece(slot, m, c, jnp.dot(zz, w2[k, :, pl.ds(c * dp_cols, dp_cols)], preferred_element_type=F32))
        else:
            d = load_full(ai, m)
            for n in range(NP):
                cs = pl.ds(n * hb, hb)
                up = lax.dot_general(d, w2[k, cs, :], NT, preferred_element_type=F32)
                gbuf[k, m, :, cs] = (gelu_d(gbuf[k, m, :, cs].astype(F32)) * up).astype(BF)
            pltpu.make_async_copy(gbuf.at[k, m], g_out.at[k, rows], outsem.at[3]).start()

            def parts():
                gg = gbuf[k, m]
                for c in range(NP):
                    emit_piece(slot, m, c, lax.dot_general(gg, w1[k, pl.ds(c * dp_cols, dp_cols), :], NT, preferred_element_type=F32))

            if slot == 3:
                pl.when(jnp.logical_not(first))(parts)
            else:
                parts()

    def do_b(slot, m):
        @pl.when(m > 0)
        def _():
            wait_in(sbuf.at[slot], ssem.at[slot])
        r = lax.rem(m, RING)
        for c in range(NP):
            wait_in(pbuf.at[slot, r, c], psem.at[slot, r, c])
            sbuf[slot, c] = (own[slot % 2, c] + pbuf[slot, r, c].astype(F32)).astype(BF)
            rcopy(sbuf.at[slot, c], qbuf.at[slot, r, c], ssem.at[slot], qsem.at[slot, r, c], other, stage).start()

    def do_c(slot, m):
        fwd = slot < 2
        k = slot if fwd else 3 - slot
        ai = k if fwd else 2 + k
        r = lax.rem(m, RING)

        @pl.when(m > 0)
        def _():
            wait_in(obuf.at[slot], oesem.at[slot])
            if slot == 1:
                @pl.when(jnp.logical_not(last))
                def _():
                    wait_in(obuf.at[slot], oosem.at[slot])
            if slot == 3:
                wait_in(obuf.at[slot], oosem.at[slot])

        for c in range(NP):
            wait_in(qbuf.at[slot, r, c], qsem.at[slot, r, c])
            h = act[ai, m, c].astype(F32) + (sbuf[slot, c].astype(F32) + qbuf[slot, r, c].astype(F32))
            h = h.astype(BF)
            if slot == 0 or slot == 2:
                di = 1 if slot == 0 else 2
                obuf[slot, c] = h
                act[di, m, c] = h
                rcopy(obuf.at[slot, c], act.at[di, m, c], oesem.at[slot], wsem.at[slot // 2, r, c], partner, stage).start()
            elif slot == 1:
                @pl.when(last)
                def _():
                    err = h.astype(F32) - tbuf[m, c].astype(F32)
                    lacc[...] += jnp.sum((err * err).reshape(n_tok // 8, 8, dp_cols), axis=0)
                    dy = (err * inv_count).astype(BF)
                    obuf[slot, c] = dy
                    act[3, m, c] = dy
                    rcopy(obuf.at[slot, c], act.at[3, m, c], oesem.at[slot], xsem.at[1, m, c], partner, stage).start()

                @pl.when(jnp.logical_not(last))
                def _():
                    obuf[slot, c] = h
                    rcopy(obuf.at[slot, c], act.at[0, m, c], oosem.at[slot], xsem.at[0, m, c], z, stage + 1).start()
                    rcopy(obuf.at[slot, c], act.at[0, m, c], oesem.at[slot], xsem.at[0, m, c], partner, stage + 1).start()
            else:
                obuf[slot, c] = h
                rcopy(obuf.at[slot, c], act.at[3, m, c], oosem.at[slot], xsem.at[1, m, c], z, stage - 1).start()
                rcopy(obuf.at[slot, c], act.at[3, m, c], oesem.at[slot], xsem.at[1, m, c], partner, stage - 1).start()

    def tick(t, carry):
        for slot in range(4):
            m = t - offs[slot]
            pl.when((m >= 0) & (m < n_micro))(functools.partial(do_a, slot, m))
            sb = (slot + 3) % 4
            mb = t - offs[sb] - (1 if slot < 1 else 0)
            ok = is_mid & (mb >= 0) & (mb < n_micro)
            if sb == 3:
                ok = ok & jnp.logical_not(first)
            pl.when(ok)(functools.partial(do_b, sb, mb))
            sc = (slot + 2) % 4
            mc = t - offs[sc] - (1 if slot < 2 else 0)
            ok = is_mid & (mc >= 0) & (mc < n_micro)
            if sc == 3:
                ok = ok & jnp.logical_not(first)
            pl.when(ok)(functools.partial(do_c, sc, mc))
        return carry

    lax.fori_loop(0, n_micro + 2 * n_layer, tick, 0)

    owner = (z == 1) & last

    @pl.when(owner)
    def _():
        ltile[...] = jnp.full(ltile.shape, jnp.sum(lacc[...]) * inv_count * 0.5, F32)
        sends = []
        for i in range(n_tp * n_stage):
            tp, pp = i // n_stage, i % n_stage
            if (tp, pp) != (1, n_stage - 1):
                sends.append(rcopy(ltile, ltile, lsend.at[i], lrecv, tp, pp))
        for s in sends:
            s.start()
        for s in sends:
            s.wait_send()

    @pl.when(jnp.logical_not(owner))
    def _():
        wait_in(ltile, lrecv)

    lout = pltpu.make_async_copy(ltile, loss_out, tsem)
    lout.start()
    lout.wait()

    for slot in range(3):
        wait_in(sbuf.at[slot], ssem.at[slot])

    @pl.when(jnp.logical_not(first))
    def _():
        wait_in(sbuf.at[3], ssem.at[3])

    @pl.when(is_mid)
    def _():
        for slot in range(3):
            wait_in(obuf.at[slot], oesem.at[slot])

        @pl.when(jnp.logical_not(last))
        def _():
            wait_in(obuf.at[1], oosem.at[1])

        @pl.when(jnp.logical_not(first))
        def _():
            wait_in(obuf.at[3], oesem.at[3])
            wait_in(obuf.at[3], oosem.at[3])

    pltpu.make_async_copy(a_out, a_out, outsem.at[0]).wait()
    pltpu.make_async_copy(d_out, d_out, outsem.at[1]).wait()
    pltpu.make_async_copy(z_out, z_out, outsem.at[2]).wait()
    pltpu.make_async_copy(g_out, g_out, outsem.at[3]).wait()


def solution(mesh):
    n_stage = mesh.shape["pp"]
    n_tp = mesh.shape["tp"]
    assert n_tp == 4

    def device_program(x_loc, y_loc, w_in, w_out):
        n_micro, n_tok, d_model = x_loc.shape
        hidden = w_in.shape[3]
        dpc = d_model // NP
        inv_count = 1.0 / (n_micro * n_tok * d_model)
        rows = n_micro * n_tok
        save_d = jax.ShapeDtypeStruct((2, rows, d_model), BF)
        save_h = jax.ShapeDtypeStruct((2, rows, hidden), BF)
        dma = pltpu.SemaphoreType.DMA
        piece = (NP, n_tok, dpc)
        a_s, d_s, g_s, z_s, loss = pl.pallas_call(
            functools.partial(step_kernel, n_stage, n_tp, inv_count),
            out_shape=(save_d, save_d, save_h, save_h, jax.ShapeDtypeStruct((8, 128), F32)),
            in_specs=[pl.BlockSpec(memory_space=pl.ANY)] * 4,
            out_specs=[pl.BlockSpec(memory_space=pl.ANY)] * 5,
            scratch_shapes=[
                pltpu.VMEM((2, d_model, hidden), BF),
                pltpu.VMEM((2, hidden, d_model), BF),
                pltpu.VMEM((4, n_micro) + piece, BF),
                pltpu.VMEM((2, n_micro, n_tok, hidden), BF),
                pltpu.VMEM((2, n_micro, n_tok, hidden), BF),
                pltpu.VMEM((4, RING) + piece, BF),
                pltpu.VMEM((4, RING) + piece, BF),
                pltpu.VMEM((4,) + piece, BF),
                pltpu.VMEM((4,) + piece, BF),
                pltpu.VMEM((2,) + piece, F32),
                pltpu.VMEM((n_micro,) + piece, BF),
                pltpu.VMEM((8, dpc), F32),
                pltpu.VMEM((8, 128), F32),
                dma((2, n_micro, NP)), dma((2, RING, NP)), dma((4, RING, NP)), dma((4, RING, NP)),
                dma((4,)), dma((4,)), dma((4,)), dma((4,)), dma, dma((4,)), dma((n_tp * n_stage,)), dma,
            ],
            compiler_params=pltpu.CompilerParams(has_side_effects=True, vmem_limit_bytes=63 * 1024 * 1024),
            name="pipeline_step",
        )(x_loc, y_loc, w_in, w_out)
        grad_first = jnp.einsum("ktd,ktf->kdf", a_s, g_s, preferred_element_type=F32)[None]
        grad_second = jnp.einsum("ktf,ktd->kfd", z_s, d_s, preferred_element_type=F32)[None]
        return grad_first, grad_second, loss[0, :1]

    return jax.shard_map(
        device_program,
        mesh=mesh,
        in_specs=(P("dp", None, None), P("dp", None, None), P("pp", None, None, "tp"), P("pp", None, "tp", None)),
        out_specs=(P(("dp", "pp"), None, None, "tp"), P(("dp", "pp"), None, "tp", None), P("dp")),
        check_vma=False,
    )
```

time: 3160 us -> 502 us (0.16)
  waiting for transfers between devices: 2270 us -> 0 us
  matrix products: 624 us -> 21.8 us
  Pallas kernels: 0 us -> 478 us
  other arithmetic: 137 us -> 0 us
  starting transfers between devices: 64.3 us -> 0 us
    psum x72 -> x0, waiting for transfers between devices: 2270 us -> none  [the longest x36 1270 us: run_tick(): branch = lax.psum(part_out, 'tp')]
    dot_general x216 -> x2, matrix products: 624 us -> 21.8 us  [the longest x1 12.8 us: device_program(): jnp.einsum('ktd,ktf->kdf', a_s, g_s, preferred_element_type=F32)[None]]
    pallas_call x0 -> x1, Pallas kernels: none -> 478 us  [device_program(): pl.pallas_call(functools.partial(step_kernel, n_stage, n_tp, inv_count),...]
    ppermute x36 -> x0, starting transfers between devices: 61.4 us -> none  [the longest x18 38.2 us: run_tick(): recv_act = lax.ppermute(cur_act, 'pp', fwd_pairs)]
    dynamic_update_slice x36 -> x0, other arithmetic: 48.2 us -> none  [run_tick(): lax.dynamic_update_index_in_dim(store_in[layer_idx], cur_act, slot_fwd, 0)]
    reduce_sum x18 -> x0, other arithmetic: 34.5 us -> none  [run_tick(): jnp.sum(error_val * error_val)]
  transfers between devices with their start and end apart: 108 -> 0, of which waited for: 72 -> 0; matrix products, arithmetic and copies ran while one was open for 17% -> 0% of each run, Pallas kernels for 0% -> 0%
where the time goes in v1:
time: 502 us
  Pallas kernels  478 us (95%)
  matrix products  21.8 us (4%)
    pallas_call x1, Pallas kernels, device_program(): pl.pallas_call(functools.partial(step_kernel, n_stage, n_tp, inv_count),...  478 us
    dot_general x1, matrix products, device_program(): jnp.einsum('ktd,ktf->kdf', a_s, g_s, preferred_element_type=F32)[None]  12.8 us

profile of v1, /device:TPU:0, one launch (start us, length us, event | category | flops | bytes accessed | tf_op | source)
XLA Modules:
  0.0 502.1 jit_solution(9480618012256827115)
XLA Ops:
  0.6 478.4 %pipeline_step.1 = (bf16[2,1536,1024]{2,1,0:T(8,128)(2,1)}, bf16[2,1536,1024]{2,1,0:T(8,128)(2,1)}, bf16[2,1536,1024]{2,1,0:T(8,128)(2,1)}, bf16[2,1536,1024]{2,1,0:T(8,128)(2,1)}, f32[8,128]{1,0:T(8,128)}) custom-call(bf16[12,128,1024]{2,1,0:T(8,128)(2,1)} %x_hbm.1, bf16[12,128,1024]{2,1,0:T(8,128)(2,1)} %t_hbm.1, bf16[1,2,1024,1024]{3,2,1,0:T(8,128)(2,1)} %w1_hbm.1, ...), custom_call_target="tpu_custom_call" | custom-call | tf_op jit(solution)/shard_map/pipeline_step/pallas_call | solution.py:297
  479.0 1.2 slice.3
  480.2 0.0 copy-start
  480.2 0.0 copy-start.1
  480.2 12.8 %convolution_bitcast_fusion.1 = f32[1,2,1024,1024]{3,2,1,0:T(8,128)} fusion(bf16[2,1536,1024]{2,1,0:T(8,128)(2,1)} %get-tuple-element.8, bf16[2,1536,1024]{2,1,0:T(8,128)(2,1)} %get-tuple-element.9), kind=kOutput, calls=%fused_computation.1 | convolution fusion | flops 6442450944 | bytes 20971520 | tf_op jit(solution)/shard_map/ktd,ktf->kdf/dot_general | solution.py:322
  493.0 0.0 copy-done
  493.0 0.0 copy-done.1
  493.0 9.0 %convolution_bitcast_fusion = f32[1,2,1024,1024]{3,2,1,0:T(8,128)} fusion(bf16[2,1536,1024]{2,1,0:T(8,128)(2,1)S(1)} %copy-done.1, bf16[2,1536,1024]{2,1,0:T(8,128)(2,1)S(1)} %copy-done), kind=kOutput, calls=%fused_computation | convolution fusion | flops 6442450944 | bytes 20971520 | tf_op jit(solution)/shard_map/ktf,ktd->kfd/dot_general | solution.py:323
Async XLA Ops:
  480.2 12.8 %copy-start = (bf16[2,1536,1024]{2,1,0:T(8,128)(2,1)S(1)}, bf16[2,1536,1024]{2,1,0:T(8,128)(2,1)}, u32[]{:S(2)}) copy-start(bf16[2,1536,1024]{2,1,0:T(8,128)(2,1)} %get-tuple-element.11) | copy-start | bytes 18874372
  480.2 12.8 %copy-start.1 = (bf16[2,1536,1024]{2,1,0:T(8,128)(2,1)S(1)}, bf16[2,1536,1024]{2,1,0:T(8,128)(2,1)}, u32[]{:S(2)}) copy-start(bf16[2,1536,1024]{2,1,0:T(8,128)(2,1)} %get-tuple-element.10) | copy-start | bytes 18874372

commit v2 on v0

v2 whole, which is shorter than its diff:
```python
import functools
import math

import jax
import jax.numpy as jnp
from jax import lax
from jax.experimental import pallas as pl
from jax.experimental.pallas import tpu as pltpu
from jax.sharding import PartitionSpec as P

BF = jnp.bfloat16
F32 = jnp.float32
NP = 4
LB, LC = 1, 2
SR = 4
WCH = 8
GC = math.sqrt(2.0 / math.pi)
NT = (((1,), (1,)), ((), ()))
MESH = pl.DeviceIdType.MESH


def gelu_f(x):
    return x * (0.5 + 0.5 * jnp.tanh(GC * (x + 0.044715 * (x * x * x))))


def gelu_d(x):
    x2 = x * x
    th = jnp.tanh(GC * (x + 0.044715 * (x * x2)))
    return 0.5 + 0.5 * th + (0.5 * x) * (1.0 - th * th) * (GC + (3 * 0.044715 * GC) * x2)


def step_kernel(n_micro, inv_count, x_hbm, t_hbm, w1_hbm, w2_hbm,
                a_out, d_out, g_out, z_out, loss_out,
                w, act, ubuf, zbuf, pbuf, qbuf, sbuf, obuf, own, lacc, ltile,
                asem, psem, qsem, ssem, oesem, oosem, ldsem, tsem, outsem, lsend, lrecv,
                wrsem, wssem, wfsem, shsem, gosem):
    nh = n_micro // 2
    n_tok, dpc = act.shape[2:]
    hid = ubuf.shape[2]
    hb = hid // NP
    nd = 3 * n_micro
    rows_w = w.shape[2] // WCH
    stage = lax.axis_index("pp")
    z = lax.axis_index("tp")
    x = lax.axis_index("dp")
    y = stage // 2
    core = lax.rem(stage, 2)
    y0, y1 = y == 0, y == 1
    c0, c1 = core == 0, core == 1
    mirror = lax.rem(stage + 2, 4)
    is_mid = (z == 1) | (z == 2)
    is_end = jnp.logical_not(is_mid)
    partner = z + 1 - 2 * lax.rem(z, 2)
    other = 3 - z
    n_slots = n_micro + 15 * nh

    def rcopy(src, dst, s_sem, r_sem, tp, pp):
        return pltpu.make_async_remote_copy(src_ref=src, dst_ref=dst, send_sem=s_sem, recv_sem=r_sem,
                                            device_id={"tp": tp, "pp": pp}, device_id_type=MESH)

    def wait_in(ref, sem):
        pltpu.make_async_copy(ref, ref, sem).wait()

    def decode(n):
        nn = jnp.maximum(n - n_micro, 0)
        r0 = n < n_micro
        rho = jnp.where(r0, 0, 1 + nn // nh)
        j = jnp.where(r0, n // 2, lax.rem(nn, nh))
        ext = r0 & (lax.rem(n + 2, 2) == 1)
        m = jnp.where(r0, j + nh * lax.rem(n + 2, 2), nh * y + j)
        fwd = rho < 8
        l = jnp.where(fwd, rho, 15 - rho)
        ok = (n >= 0) & (n < n_slots) & (lax.rem(l // 2, 2) == core)
        ok = ok & (y0 | ((rho > 0) & (rho < 15)))
        return dict(n=n, rho=rho, j=j, ext=ext, m=m, fwd=fwd, l=l, ok=ok, ar=ok & (rho < 15))

    def index_of(l, m, j, yy):
        home = (l // 4) == yy
        return jnp.where(home, lax.rem(l, 2) * n_micro + m, 2 * n_micro + lax.rem(l, 2) * nh + j)

    def p_slot(e):
        return jnp.where(e["ext"], nh + e["j"], e["j"])

    def q_slot(e):
        return jnp.where(e["ext"], 2 * nh + e["j"], lax.rem(e["rho"], 2) * nh + e["j"])

    def dest(e):
        l, m, j, fwd = e["l"], e["m"], e["j"], e["fwd"]
        last = fwd & (l == 7)
        dl = jnp.where(fwd, jnp.where(last, 7, l + 1), l - 1)
        dy = jnp.where(e["ext"], 1, jnp.where(jnp.logical_not(fwd) & (l == 1), 0, y))
        dc = lax.rem(dl // 2, 2)
        grad = last | jnp.logical_not(fwd)
        di = index_of(dl, m, j, dy) + jnp.where(grad, nd, 0)
        return last, di, 2 * dy + dc, (dy == y) & (dc == core)

    loads = []
    for k in range(2):
        loads.append(pltpu.make_async_copy(w1_hbm.at[0, k], w.at[2 * y + k, 0], ldsem.at[k]))
        loads.append(pltpu.make_async_copy(w2_hbm.at[0, k], w.at[2 * y + k, 1], ldsem.at[2 + k]))
    for ld in loads:
        ld.start()

    @pl.when(y0 & c0)
    def _():
        @pl.loop(0, n_micro)
        def _(m):
            for c in range(NP):
                pltpu.make_async_copy(x_hbm.at[m, :, pl.ds(c * dpc, dpc)], act.at[m, c], asem.at[m, c]).start()

    lacc[...] = jnp.zeros_like(lacc)
    t_base = nd + index_of(7, nh * y, 0, y)

    @pl.when(c1 & is_mid)
    def _():
        @pl.loop(0, nh)
        def _(j):
            for c in range(NP):
                pltpu.make_async_copy(t_hbm.at[nh * y + j, :, pl.ds(c * dpc, dpc)], act.at[t_base + j, c], tsem).start()
        wait_in(act.at[pl.ds(t_base, nh)], tsem)

    for ld in loads:
        ld.wait()

    def send_weights(k):
        for i in range(WCH):
            half, g = i // (WCH // 2), lax.rem(2 * i, WCH) + x
            src = w.at[2 * y + k, half, pl.ds(g * rows_w, rows_w)]
            rcopy(src, src, wssem, wrsem.at[k, half, g], z, mirror).start()

    pl.when(jnp.logical_not(y0))(functools.partial(send_weights, 0))
    pl.when(c0 | y1)(functools.partial(send_weights, 1))

    @pl.when(y0 & c1)
    def _():
        pl.semaphore_wait(gosem, 1)
        send_weights(0)
        send_weights(1)

    n_chunk = jnp.where(y1 & c0, WCH, 2 * WCH)
    relay0 = jnp.where(y0, jnp.where(c0, 2, 26), jnp.where(c0, 0, 8))

    def relay(i):
        k = jnp.where(y1 & c0, 1, i // WCH)
        i = lax.rem(i, WCH)
        half = i // (WCH // 2)
        g = lax.rem(2 * i, WCH) + x
        ref = w.at[2 * (1 - y) + k, half, pl.ds(pl.multiple_of(g * rows_w, rows_w), rows_w)]
        wait_in(ref, wrsem.at[k, half, g])
        pltpu.make_async_remote_copy(src_ref=ref, dst_ref=ref, send_sem=wfsem, recv_sem=wrsem.at[k, half, g],
                                     device_id={"dp": 1 - x}, device_id_type=MESH).start()

    def wait_weights(k):
        for i in range(WCH):
            half, g = i // (WCH // 2), lax.rem(2 * i, WCH) + (1 - x)
            ref = w.at[2 * (1 - y) + k, half, pl.ds(pl.multiple_of(g * rows_w, rows_w), rows_w)]
            wait_in(ref, wrsem.at[k, half, g])

    def load_full(ai):
        return jnp.concatenate([act[ai, c] for c in range(NP)], axis=1)

    def put_act(ai, k, m, dst, sem):
        for c in range(NP):
            pltpu.make_async_copy(act.at[ai, c], dst.at[k, pl.ds(pl.multiple_of(m * n_tok, n_tok), n_tok), pl.ds(c * dpc, dpc)], sem).start()

    def put_hid(src, k, m, dst, sem):
        pltpu.make_async_copy(src, dst.at[k, pl.ds(pl.multiple_of(m * n_tok, n_tok), n_tok)], sem).start()

    def ship(ai, hi):
        rcopy(act.at[ai], act.at[hi], shsem, asem.at[hi, 0], z, mirror).start()

    def up_fwd(ai, wi, zi):
        a = load_full(ai)
        for n in range(NP):
            cs = pl.ds(n * hb, hb)
            u = jnp.dot(a, w[wi, 0, :, cs], preferred_element_type=F32).astype(BF)
            ubuf[ai, :, cs] = u
            zbuf[zi, :, cs] = gelu_f(u.astype(F32)).astype(BF)

    def up_bwd(ai, wi):
        d = load_full(nd + ai)
        for n in range(NP):
            cs = pl.ds(n * hb, hb)
            up = lax.dot_general(d, w[wi, 1, cs, :], NT, preferred_element_type=F32)
            ubuf[ai, :, cs] = (gelu_d(ubuf[ai, :, cs].astype(F32)) * up).astype(BF)

    def emit_piece(e, c, part):
        @pl.when(is_end)
        def _():
            s, r = lax.rem(e["n"], SR), p_slot(e)
            sbuf[s, c] = part.astype(BF)
            rcopy(sbuf.at[s, c], pbuf.at[r, c], ssem.at[s], psem.at[r, c], partner, stage).start()

        @pl.when(is_mid)
        def _():
            own[lax.rem(e["n"], LB + 1), c] = part

    def do_a(e):
        l, m, j, fwd = e["l"], e["m"], e["j"], e["fwd"]
        k = lax.rem(l, 2)
        home = (l // 4) == y
        wi = 2 * (l // 4) + k
        ai = index_of(l, m, j, y)
        hi = k * n_micro + m
        odd = k == 1

        @pl.when(fwd)
        def _():
            @pl.when(is_end | (k == 0) | ((l == 1) & y1))
            def _():
                for c in range(NP):
                    wait_in(act.at[ai, c], asem.at[ai, c])

            @pl.when(jnp.logical_not(home))
            def _():
                ship(ai, hi)
                pl.when(j == 0)(functools.partial(wait_weights, k))

            zi = jnp.where(home, hi, 2 * n_micro)
            up_fwd(ai, wi, zi)

            @pl.when(home)
            def _():
                put_act(ai, k, m, a_out, outsem.at[0])
                put_hid(zbuf.at[zi], k, m, z_out, outsem.at[2])

            zz = zbuf[zi]
            for c in range(NP):
                emit_piece(e, c, jnp.dot(zz, w[wi, 1, :, pl.ds(c * dpc, dpc)], preferred_element_type=F32))

        @pl.when(jnp.logical_not(fwd))
        def _():
            @pl.when(is_end | (odd & (l < 7)))
            def _():
                for c in range(NP):
                    wait_in(act.at[nd + ai, c], asem.at[nd + ai, c])

            pl.when(jnp.logical_not(home))(functools.partial(ship, nd + ai, nd + hi))
            up_bwd(ai, wi)

            @pl.when(home)
            def _():
                put_act(nd + ai, k, m, d_out, outsem.at[1])
                put_hid(ubuf.at[ai], k, m, g_out, outsem.at[3])

            @pl.when(e["ar"])
            def _():
                gg = ubuf[ai]
                for c in range(NP):
                    emit_piece(e, c, lax.dot_general(gg, w[wi, 0, pl.ds(c * dpc, dpc), :], NT, preferred_element_type=F32))

    def do_b(e):
        s, r, qr = lax.rem(e["n"], SR), p_slot(e), q_slot(e)
        so = lax.rem(e["n"], LB + 1)
        for c in range(NP):
            wait_in(pbuf.at[r, c], psem.at[r, c])
            sbuf[s, c] = (own[so, c] + pbuf[r, c].astype(F32)).astype(BF)
            rcopy(sbuf.at[s, c], qbuf.at[qr, c], ssem.at[s], qsem.at[qr, c], other, stage).start()

    def do_c(e):
        s, qr = lax.rem(e["n"], SR), q_slot(e)
        ai = index_of(e["l"], e["m"], e["j"], y) + jnp.where(e["fwd"], 0, nd)
        last, di, ds, local = dest(e)
        for c in range(NP):
            wait_in(qbuf.at[qr, c], qsem.at[qr, c])
            h = act[ai, c].astype(F32) + (sbuf[s, c].astype(F32) + qbuf[qr, c].astype(F32))
            h = h.astype(BF)

            @pl.when(last)
            def _():
                err = h.astype(F32) - act[di, c].astype(F32)
                lacc[...] += jnp.sum((err * err).reshape(n_tok // 8, 8, dpc), axis=0)
                dy = (err * inv_count).astype(BF)
                obuf[s, c] = dy
                act[di, c] = dy

            @pl.when(jnp.logical_not(last))
            def _():
                obuf[s, c] = h

                @pl.when(local)
                def _():
                    act[di, c] = h

            @pl.when(jnp.logical_not(local))
            def _():
                rcopy(obuf.at[s, c], act.at[di, c], oosem.at[s], asem.at[di, c], z, ds).start()

            rcopy(obuf.at[s, c], act.at[di, c], oesem.at[s], asem.at[di, c], partner, ds).start()

    redo0 = jnp.where(y0, jnp.where(c0, n_slots - nh, n_slots - 2 * nh), jnp.where(c0, n_slots - 4 * nh, n_slots - 6 * nh))

    def redo(i):
        k = 1 - i // nh
        m = nh * (1 - y) + lax.rem(i, nh)
        hi = k * n_micro + m
        wi = 2 * y + k
        layer0 = y0 & c0 & (k == 0)

        @pl.when(jnp.logical_not(layer0))
        def _():
            wait_in(act.at[hi], asem.at[hi, 0])
            wait_in(act.at[nd + hi], asem.at[nd + hi, 0])
            put_act(hi, k, m, a_out, outsem.at[0])
            up_fwd(hi, wi, hi)
            put_hid(zbuf.at[hi], k, m, z_out, outsem.at[2])

        @pl.when(layer0)
        def _():
            for c in range(NP):
                wait_in(act.at[nd + hi, c], asem.at[nd + hi, c])

        put_act(nd + hi, k, m, d_out, outsem.at[1])
        up_bwd(hi, wi)
        put_hid(ubuf.at[hi], k, m, g_out, outsem.at[3])

    def slot(n, carry):
        e = decode(n)
        old = decode(n - SR)
        eb, ebo = decode(n - LB), decode(n - LB - SR)
        ec, eco = decode(n - LC), decode(n - LC - SR)

        @pl.when((is_end & old["ar"]) | (is_mid & ebo["ar"]))
        def _():
            s = lax.rem(n + SR - jnp.where(is_end, 0, LB), SR)
            wait_in(sbuf.at[s], ssem.at[s])

        @pl.when(is_mid & eco["ar"])
        def _():
            s = lax.rem(n + SR - LC, SR)
            wait_in(obuf.at[s], oesem.at[s])
            local = dest(eco)[3]
            pl.when(jnp.logical_not(local))(lambda: wait_in(obuf.at[s], oosem.at[s]))

        pl.when(e["ok"])(functools.partial(do_a, e))
        pl.when(is_mid & eb["ar"])(functools.partial(do_b, eb))
        pl.when(is_mid & ec["ar"])(functools.partial(do_c, ec))
        ri = n - relay0
        pl.when((ri >= 0) & (ri < n_chunk))(functools.partial(relay, ri))

        @pl.when(y0 & c0 & (n == 8))
        def _():
            wait_in(w.at[1, 0], wssem)
            pl.semaphore_signal(gosem, 1, device_id={"pp": 1}, device_id_type=MESH)

        di = n - redo0
        pl.when((di >= 0) & (di < 2 * nh))(functools.partial(redo, di))
        return carry

    lax.fori_loop(0, n_slots + LC + SR + 2, slot, 0)

    owner = (z == 1) & c1

    @pl.when(owner)
    def _():
        ltile[y] = jnp.full(ltile.shape[1:], jnp.sum(lacc[...]) * inv_count * 0.5, F32)
        for i in range(16):
            tp, pp = i // 4, i % 4

            @pl.when((tp != 1) | (pp != stage))
            def _():
                rcopy(ltile.at[y], ltile.at[y], lsend.at[i], lrecv.at[y], tp, pp).start()
        for i in range(16):
            tp, pp = i // 4, i % 4

            @pl.when((tp != 1) | (pp != stage))
            def _():
                wait_in(ltile.at[y], lsend.at[i])

    for yy in range(2):
        @pl.when(jnp.logical_not(owner & (y == yy)))
        def _():
            wait_in(ltile.at[yy], lrecv.at[yy])

    ltile[0] = ltile[0] + ltile[1]
    lout = pltpu.make_async_copy(ltile.at[0], loss_out, tsem)
    lout.start()
    lout.wait()

    for full, sem in ((jnp.logical_not(y0 & c0), wssem), (jnp.logical_not(y1 & c0), wfsem)):
        pl.when(full)(functools.partial(wait_in, w.at[0], sem))
    pl.when(y1 & c0)(functools.partial(wait_in, w.at[0, 0], wfsem))
    half_ship = y1 & c0
    pl.when(half_ship)(functools.partial(wait_in, act.at[pl.ds(0, n_micro)], shsem))
    pl.when(jnp.logical_not(half_ship))(functools.partial(wait_in, act.at[pl.ds(0, 2 * n_micro)], shsem))
    pltpu.make_async_copy(a_out, a_out, outsem.at[0]).wait()
    pltpu.make_async_copy(d_out, d_out, outsem.at[1]).wait()
    pltpu.make_async_copy(z_out, z_out, outsem.at[2]).wait()
    pltpu.make_async_copy(g_out, g_out, outsem.at[3]).wait()


def solution(mesh):
    assert (mesh.shape["tp"], mesh.shape["pp"], mesh.shape["dp"]) == (4, 4, 2)

    def device_program(x_loc, y_loc, w_in, w_out):
        n_micro, n_tok, d_model = x_loc.shape
        hidden = w_in.shape[3]
        assert d_model == hidden and n_micro % 2 == 0
        dpc = d_model // NP
        nh = n_micro // 2
        inv_count = 1.0 / (n_micro * n_tok * d_model)
        rows = n_micro * n_tok
        save_d = jax.ShapeDtypeStruct((2, rows, d_model), BF)
        save_h = jax.ShapeDtypeStruct((2, rows, hidden), BF)
        dma = pltpu.SemaphoreType.DMA
        piece = (NP, n_tok, dpc)
        a_s, d_s, g_s, z_s, loss = pl.pallas_call(
            functools.partial(step_kernel, n_micro, inv_count),
            out_shape=(save_d, save_d, save_h, save_h, jax.ShapeDtypeStruct((8, 128), F32)),
            in_specs=[pl.BlockSpec(memory_space=pl.ANY)] * 4,
            out_specs=[pl.BlockSpec(memory_space=pl.ANY)] * 5,
            scratch_shapes=[
                pltpu.VMEM((4, 2, d_model, hidden), BF),
                pltpu.VMEM((6 * n_micro,) + piece, BF),
                pltpu.VMEM((3 * n_micro, n_tok, hidden), BF),
                pltpu.VMEM((2 * n_micro + 1, n_tok, hidden), BF),
                pltpu.VMEM((2 * nh,) + piece, BF),
                pltpu.VMEM((3 * nh,) + piece, BF),
                pltpu.VMEM((SR,) + piece, BF),
                pltpu.VMEM((SR,) + piece, BF),
                pltpu.VMEM((LB + 1,) + piece, F32),
                pltpu.VMEM((8, dpc), F32),
                pltpu.VMEM((2, 8, 128), F32),
                dma((6 * n_micro, NP)), dma((2 * nh, NP)), dma((3 * nh, NP)),
                dma((SR,)), dma((SR,)), dma((SR,)), dma((4,)), dma, dma((4,)), dma((16,)), dma((2,)),
                dma((2, 2, WCH)), dma, dma, dma, pltpu.SemaphoreType.REGULAR,
            ],
            compiler_params=pltpu.CompilerParams(has_side_effects=True, vmem_limit_bytes=67043328),
            name="pipeline_step",
        )(x_loc, y_loc, w_in, w_out)
        grad_first = jnp.einsum("ktd,ktf->kdf", a_s, g_s, preferred_element_type=F32)[None]
        grad_second = jnp.einsum("ktf,ktd->kfd", z_s, d_s, preferred_element_type=F32)[None]
        return grad_first, grad_second, loss[0, :1]

    return jax.shard_map(
        device_program,
        mesh=mesh,
        in_specs=(P("dp", None, None), P("dp", None, None), P("pp", None, None, "tp"), P("pp", None, "tp", None)),
        out_specs=(P(("dp", "pp"), None, None, "tp"), P(("dp", "pp"), None, "tp", None), P("dp")),
        check_vma=False,
    )
```

time: 3160 us -> 425 us (0.13)
  waiting for transfers between devices: 2270 us -> 0 us
  matrix products: 624 us -> 21.8 us
  Pallas kernels: 0 us -> 399 us
  other arithmetic: 137 us -> 0 us
  starting transfers between devices: 64.3 us -> 0 us
    psum x72 -> x0, waiting for transfers between devices: 2270 us -> none  [the longest x36 1270 us: run_tick(): branch = lax.psum(part_out, 'tp')]
    dot_general x216 -> x2, matrix products: 624 us -> 21.8 us  [the longest x1 12.8 us: device_program(): jnp.einsum('ktd,ktf->kdf', a_s, g_s, preferred_element_type=F32)[None]]
    pallas_call x0 -> x1, Pallas kernels: none -> 399 us  [device_program(): pl.pallas_call(functools.partial(step_kernel, n_micro, inv_count), out_sh...]
    ppermute x36 -> x0, starting transfers between devices: 61.4 us -> none  [the longest x18 38.2 us: run_tick(): recv_act = lax.ppermute(cur_act, 'pp', fwd_pairs)]
    dynamic_update_slice x36 -> x0, other arithmetic: 48.2 us -> none  [run_tick(): lax.dynamic_update_index_in_dim(store_in[layer_idx], cur_act, slot_fwd, 0)]
    reduce_sum x18 -> x0, other arithmetic: 34.5 us -> none  [run_tick(): jnp.sum(error_val * error_val)]
  transfers between devices with their start and end apart: 108 -> 0, of which waited for: 72 -> 0; matrix products, arithmetic and copies ran while one was open for 17% -> 0% of each run, Pallas kernels for 0% -> 0%
where the time goes in v2:
time: 425 us; the launch traced here: 423 us
  Pallas kernels  399 us (94%)
  matrix products  21.8 us (5%)
    pallas_call x1, Pallas kernels, device_program(): pl.pallas_call(functools.partial(step_kernel, n_micro, inv_count), out_sh...  399 us
    dot_general x1, matrix products, device_program(): jnp.einsum('ktd,ktf->kdf', a_s, g_s, preferred_element_type=F32)[None]  12.8 us
    dot_general x1, matrix products, device_program(): jnp.einsum('ktf,ktd->kfd', z_s, d_s, preferred_element_type=F32)[None]  9 us

profile of v2, /device:TPU:0, one launch (start us, length us, event | category | flops | bytes accessed | tf_op | source)
XLA Modules:
  0.0 422.8 jit_solution(4542289503570538763)
XLA Ops:
  0.6 399.2 %pipeline_step.1 = (bf16[2,1536,1024]{2,1,0:T(8,128)(2,1)}, bf16[2,1536,1024]{2,1,0:T(8,128)(2,1)}, bf16[2,1536,1024]{2,1,0:T(8,128)(2,1)}, bf16[2,1536,1024]{2,1,0:T(8,128)(2,1)}, f32[8,128]{1,0:T(8,128)}) custom-call(bf16[12,128,1024]{2,1,0:T(8,128)(2,1)} %x_hbm.1, bf16[12,128,1024]{2,1,0:T(8,128)(2,1)} %t_hbm.1, bf16[1,2,1024,1024]{3,2,1,0:T(8,128)(2,1)} %w1_hbm.1, ...), custom_call_target="tpu_custom_call" | custom-call | tf_op jit(solution)/shard_map/pipeline_step/pallas_call | solution.py:407
  399.8 1.2 slice.3
  401.0 0.0 copy-start
  401.0 0.0 copy-start.1
  401.0 12.8 %convolution_bitcast_fusion.1 = f32[1,2,1024,1024]{3,2,1,0:T(8,128)} fusion(bf16[2,1536,1024]{2,1,0:T(8,128)(2,1)} %get-tuple-element.8, bf16[2,1536,1024]{2,1,0:T(8,128)(2,1)} %get-tuple-element.9), kind=kOutput, calls=%fused_computation.1 | convolution fusion | flops 6442450944 | bytes 20971520 | tf_op jit(solution)/shard_map/ktd,ktf->kdf/dot_general | solution.py:431
  413.8 0.0 copy-done
  413.8 0.0 copy-done.1
  413.8 9.0 %convolution_bitcast_fusion = f32[1,2,1024,1024]{3,2,1,0:T(8,128)} fusion(bf16[2,1536,1024]{2,1,0:T(8,128)(2,1)S(1)} %copy-done.1, bf16[2,1536,1024]{2,1,0:T(8,128)(2,1)S(1)} %copy-done), kind=kOutput, calls=%fused_computation | convolution fusion | flops 6442450944 | bytes 20971520 | tf_op jit(solution)/shard_map/ktf,ktd->kfd/dot_general | solution.py:432
Async XLA Ops:
  401.0 12.8 %copy-start = (bf16[2,1536,1024]{2,1,0:T(8,128)(2,1)S(1)}, bf16[2,1536,1024]{2,1,0:T(8,128)(2,1)}, u32[]{:S(2)}) copy-start(bf16[2,1536,1024]{2,1,0:T(8,128)(2,1)} %get-tuple-element.11) | copy-start | bytes 18874372
  401.0 12.8 %copy-start.1 = (bf16[2,1536,1024]{2,1,0:T(8,128)(2,1)S(1)}, bf16[2,1536,1024]{2,1,0:T(8,128)(2,1)}, u32[]{:S(2)}) copy-start(bf16[2,1536,1024]{2,1,0:T(8,128)(2,1)} %get-tuple-element.10) | copy-start | bytes 18874372

commit v3 on v2

--- a/solution.py
+++ b/solution.py
@@ -10,8 +10,9 @@
 
 BF = jnp.bfloat16
 F32 = jnp.float32
-NP = 4
-LB, LC = 1, 2
+NP = 2
+FB, BB, EF, EB = 4, 8, 4, 8
+LB, LC = 1, 3
 SR = 4
 WCH = 8
 GC = math.sqrt(2.0 / math.pi)
@@ -33,11 +34,10 @@
                 a_out, d_out, g_out, z_out, loss_out,
                 w, act, ubuf, zbuf, pbuf, qbuf, sbuf, obuf, own, lacc, ltile,
                 asem, psem, qsem, ssem, oesem, oosem, ldsem, tsem, outsem, lsend, lrecv,
-                wrsem, wssem, wfsem, shsem, gosem):
+                wrsem, wssem, wfsem, shsem, pxsem, gosem):
     nh = n_micro // 2
     n_tok, dpc = act.shape[2:]
     hid = ubuf.shape[2]
-    hb = hid // NP
     nd = 3 * n_micro
     rows_w = w.shape[2] // WCH
     stage = lax.axis_index("pp")
@@ -65,9 +65,9 @@
         nn = jnp.maximum(n - n_micro, 0)
         r0 = n < n_micro
         rho = jnp.where(r0, 0, 1 + nn // nh)
-        j = jnp.where(r0, n // 2, lax.rem(nn, nh))
-        ext = r0 & (lax.rem(n + 2, 2) == 1)
-        m = jnp.where(r0, j + nh * lax.rem(n + 2, 2), nh * y + j)
+        ext = n < nh
+        j = jnp.where(r0, jnp.where(ext, n, n - nh), lax.rem(nn, nh))
+        m = jnp.where(r0, jnp.where(ext, n + nh, n - nh), nh * y + j)
         fwd = rho < 8
         l = jnp.where(fwd, rho, 15 - rho)
         ok = (n >= 0) & (n < n_slots) & (lax.rem(l // 2, 2) == core)
@@ -140,6 +140,11 @@
     n_chunk = jnp.where(y1 & c0, WCH, 2 * WCH)
     relay0 = jnp.where(y0, jnp.where(c0, 2, 26), jnp.where(c0, 0, 8))
 
+    def relayed(n):
+        late = jnp.where(n < 19, jnp.clip(n - relay0, 0, WCH), jnp.where(n < 24, n - 11, 2 * WCH))
+        slow = jnp.clip((n - 4) // 2, 0, n_chunk)
+        return jnp.where(y1 & c1 & (n > 8), late, jnp.where(y0 & c0, slow, jnp.clip(n - relay0, 0, n_chunk)))
+
     def relay(i):
         k = jnp.where(y1 & c0, 1, i // WCH)
         i = lax.rem(i, WCH)
@@ -171,7 +176,8 @@
 
     def up_fwd(ai, wi, zi):
         a = load_full(ai)
-        for n in range(NP):
+        hb = hid // FB
+        for n in range(FB):
             cs = pl.ds(n * hb, hb)
             u = jnp.dot(a, w[wi, 0, :, cs], preferred_element_type=F32).astype(BF)
             ubuf[ai, :, cs] = u
@@ -179,21 +185,28 @@
 
     def up_bwd(ai, wi):
         d = load_full(nd + ai)
-        for n in range(NP):
+        hb = hid // BB
+        for n in range(BB):
             cs = pl.ds(n * hb, hb)
             up = lax.dot_general(d, w[wi, 1, cs, :], NT, preferred_element_type=F32)
             ubuf[ai, :, cs] = (gelu_d(ubuf[ai, :, cs].astype(F32)) * up).astype(BF)
 
-    def emit_piece(e, c, part):
-        @pl.when(is_end)
-        def _():
-            s, r = lax.rem(e["n"], SR), p_slot(e)
-            sbuf[s, c] = part.astype(BF)
-            rcopy(sbuf.at[s, c], pbuf.at[r, c], ssem.at[s], psem.at[r, c], partner, stage).start()
-
-        @pl.when(is_mid)
-        def _():
-            own[lax.rem(e["n"], LB + 1), c] = part
+    def emit(e, nb, product):
+        bw, per = dpc * NP // nb, nb // NP
+        for c in range(NP):
+            parts = [product(pl.ds((c * per + i) * bw, bw)) for i in range(per)]
+
+            @pl.when(is_end)
+            def _():
+                s, r = lax.rem(e["n"], SR), p_slot(e)
+                for i, part in enumerate(parts):
+                    sbuf[s, c, :, pl.ds(i * bw, bw)] = part.astype(BF)
+                rcopy(sbuf.at[s, c], pbuf.at[r, c], ssem.at[s], psem.at[r, c], partner, stage).start()
+
+            @pl.when(is_mid)
+            def _():
+                for i, part in enumerate(parts):
+                    own[lax.rem(e["n"], LB + 1), c, :, pl.ds(i * bw, bw)] = part
 
     def do_a(e):
         l, m, j, fwd = e["l"], e["m"], e["j"], e["fwd"]
@@ -211,6 +224,10 @@
                 for c in range(NP):
                     wait_in(act.at[ai, c], asem.at[ai, c])
 
+                    @pl.when(is_mid & (l == 1))
+                    def _():
+                        rcopy(act.at[ai, c], act.at[ai, c], pxsem, asem.at[ai, c], partner, stage).start()
+
             @pl.when(jnp.logical_not(home))
             def _():
                 ship(ai, hi)
@@ -225,8 +242,7 @@
                 put_hid(zbuf.at[zi], k, m, z_out, outsem.at[2])
 
             zz = zbuf[zi]
-            for c in range(NP):
-                emit_piece(e, c, jnp.dot(zz, w[wi, 1, :, pl.ds(c * dpc, dpc)], preferred_element_type=F32))
+            emit(e, EF, lambda cs: jnp.dot(zz, w[wi, 1, :, cs], preferred_element_type=F32))
 
         @pl.when(jnp.logical_not(fwd))
         def _():
@@ -246,8 +262,7 @@
             @pl.when(e["ar"])
             def _():
                 gg = ubuf[ai]
-                for c in range(NP):
-                    emit_piece(e, c, lax.dot_general(gg, w[wi, 0, pl.ds(c * dpc, dpc), :], NT, preferred_element_type=F32))
+                emit(e, EB, lambda cs: lax.dot_general(gg, w[wi, 0, cs, :], NT, preferred_element_type=F32))
 
     def do_b(e):
         s, r, qr = lax.rem(e["n"], SR), p_slot(e), q_slot(e)
@@ -286,24 +301,33 @@
             def _():
                 rcopy(obuf.at[s, c], act.at[di, c], oosem.at[s], asem.at[di, c], z, ds).start()
 
-            rcopy(obuf.at[s, c], act.at[di, c], oesem.at[s], asem.at[di, c], partner, ds).start()
-
-    redo0 = jnp.where(y0, jnp.where(c0, n_slots - nh, n_slots - 2 * nh), jnp.where(c0, n_slots - 4 * nh, n_slots - 6 * nh))
-
-    def redo(i):
+            @pl.when(jnp.logical_not(e["ext"]))
+            def _():
+                rcopy(obuf.at[s, c], act.at[di, c], oesem.at[s], asem.at[di, c], partner, ds).start()
+
+    redo_b0 = jnp.where(y0, jnp.where(c0, n_slots - nh, n_slots - 2 * nh), jnp.where(c0, n_slots - 4 * nh, n_slots - 6 * nh))
+    redo_f0 = jnp.where(y0, jnp.where(c0, n_slots - 9 * nh, n_slots - 6 * nh), jnp.where(c0, n_slots - 8 * nh, n_slots - 6 * nh))
+    n_redo_f = jnp.where(y0 & c0, nh, 2 * nh)
+
+    def redo_at(i):
         k = 1 - i // nh
         m = nh * (1 - y) + lax.rem(i, nh)
-        hi = k * n_micro + m
-        wi = 2 * y + k
+        return k, m, k * n_micro + m, 2 * y + k
+
+    def redo_f(i):
+        k, m, hi, wi = redo_at(i)
+        wait_in(act.at[hi], asem.at[hi, 0])
+        put_act(hi, k, m, a_out, outsem.at[0])
+        up_fwd(hi, wi, hi)
+        put_hid(zbuf.at[hi], k, m, z_out, outsem.at[2])
+
+    def redo_b(i):
+        k, m, hi, wi = redo_at(i)
         layer0 = y0 & c0 & (k == 0)
 
         @pl.when(jnp.logical_not(layer0))
         def _():
-            wait_in(act.at[hi], asem.at[hi, 0])
             wait_in(act.at[nd + hi], asem.at[nd + hi, 0])
-            put_act(hi, k, m, a_out, outsem.at[0])
-            up_fwd(hi, wi, hi)
-            put_hid(zbuf.at[hi], k, m, z_out, outsem.at[2])
 
         @pl.when(layer0)
         def _():
@@ -328,23 +352,27 @@
         @pl.when(is_mid & eco["ar"])
         def _():
             s = lax.rem(n + SR - LC, SR)
-            wait_in(obuf.at[s], oesem.at[s])
+            pl.when(jnp.logical_not(eco["ext"]))(lambda: wait_in(obuf.at[s], oesem.at[s]))
             local = dest(eco)[3]
             pl.when(jnp.logical_not(local))(lambda: wait_in(obuf.at[s], oosem.at[s]))
 
+        @pl.loop(relayed(n), relayed(n + 1))
+        def _(i):
+            relay(i)
+
         pl.when(e["ok"])(functools.partial(do_a, e))
+        pl.when(is_mid & ec["ar"])(functools.partial(do_c, ec))
         pl.when(is_mid & eb["ar"])(functools.partial(do_b, eb))
-        pl.when(is_mid & ec["ar"])(functools.partial(do_c, ec))
-        ri = n - relay0
-        pl.when((ri >= 0) & (ri < n_chunk))(functools.partial(relay, ri))
-
-        @pl.when(y0 & c0 & (n == 8))
+
+        @pl.when(y0 & c0 & (n == 6))
         def _():
             wait_in(w.at[1, 0], wssem)
             pl.semaphore_signal(gosem, 1, device_id={"pp": 1}, device_id_type=MESH)
 
-        di = n - redo0
-        pl.when((di >= 0) & (di < 2 * nh))(functools.partial(redo, di))
+        fi = n - redo_f0
+        pl.when((fi >= 0) & (fi < n_redo_f))(functools.partial(redo_f, fi))
+        bi = n - redo_b0
+        pl.when((bi >= 0) & (bi < 2 * nh))(functools.partial(redo_b, bi))
         return carry
 
     lax.fori_loop(0, n_slots + LC + SR + 2, slot, 0)
@@ -380,6 +408,7 @@
     for full, sem in ((jnp.logical_not(y0 & c0), wssem), (jnp.logical_not(y1 & c0), wfsem)):
         pl.when(full)(functools.partial(wait_in, w.at[0], sem))
     pl.when(y1 & c0)(functools.partial(wait_in, w.at[0, 0], wfsem))
+    pl.when(y1 & c0 & is_mid)(functools.partial(wait_in, act.at[pl.ds(0, nh)], pxsem))
     half_ship = y1 & c0
     pl.when(half_ship)(functools.partial(wait_in, act.at[pl.ds(0, n_micro)], shsem))
     pl.when(jnp.logical_not(half_ship))(functools.partial(wait_in, act.at[pl.ds(0, 2 * n_micro)], shsem))
@@ -423,7 +452,7 @@
                 pltpu.VMEM((2, 8, 128), F32),
                 dma((6 * n_micro, NP)), dma((2 * nh, NP)), dma((3 * nh, NP)),
                 dma((SR,)), dma((SR,)), dma((SR,)), dma((4,)), dma, dma((4,)), dma((16,)), dma((2,)),
-                dma((2, 2, WCH)), dma, dma, dma, pltpu.SemaphoreType.REGULAR,
+                dma((2, 2, WCH)), dma, dma, dma, dma, pltpu.SemaphoreType.REGULAR,
             ],
             compiler_params=pltpu.CompilerParams(has_side_effects=True, vmem_limit_bytes=67043328),
             name="pipeline_step",

time: 425 us -> 362 us (0.85)
  Pallas kernels: 399 us -> 338 us
    pallas_call x1, Pallas kernels: 399 us -> 338 us  [device_program(): pl.pallas_call(functools.partial(step_kernel, n_micro, inv_count), out_sh...]
where the time goes in v3:
time: 362 us
  Pallas kernels  338 us (93%)
  matrix products  21.8 us (6%)
    pallas_call x1, Pallas kernels, device_program(): pl.pallas_call(functools.partial(step_kernel, n_micro, inv_count), out_sh...  338 us
    dot_general x1, matrix products, device_program(): jnp.einsum('ktd,ktf->kdf', a_s, g_s, preferred_element_type=F32)[None]  12.8 us
    dot_general x1, matrix products, device_program(): jnp.einsum('ktf,ktd->kfd', z_s, d_s, preferred_element_type=F32)[None]  8.99 us

profile of v3, /device:TPU:0, one launch (start us, length us, event | category | flops | bytes accessed | tf_op | source)
XLA Modules:
  0.0 361.7 jit_solution(8645020870962630708)
XLA Ops:
  0.6 338.1 %pipeline_step.1 = (bf16[2,1536,1024]{2,1,0:T(8,128)(2,1)}, bf16[2,1536,1024]{2,1,0:T(8,128)(2,1)}, bf16[2,1536,1024]{2,1,0:T(8,128)(2,1)}, bf16[2,1536,1024]{2,1,0:T(8,128)(2,1)}, f32[8,128]{1,0:T(8,128)}) custom-call(bf16[12,128,1024]{2,1,0:T(8,128)(2,1)} %x_hbm.1, bf16[12,128,1024]{2,1,0:T(8,128)(2,1)} %t_hbm.1, bf16[1,2,1024,1024]{3,2,1,0:T(8,128)(2,1)} %w1_hbm.1, ...), custom_call_target="tpu_custom_call" | custom-call | tf_op jit(solution)/shard_map/pipeline_step/pallas_call | solution.py:436
  338.7 1.2 slice.3
  339.9 0.0 copy-start
  339.9 0.0 copy-start.1
  339.9 12.8 %convolution_bitcast_fusion.1 = f32[1,2,1024,1024]{3,2,1,0:T(8,128)} fusion(bf16[2,1536,1024]{2,1,0:T(8,128)(2,1)} %get-tuple-element.8, bf16[2,1536,1024]{2,1,0:T(8,128)(2,1)} %get-tuple-element.9), kind=kOutput, calls=%fused_computation.1 | convolution fusion | flops 6442450944 | bytes 20971520 | tf_op jit(solution)/shard_map/ktd,ktf->kdf/dot_general | solution.py:460
  352.7 0.0 copy-done
  352.7 0.0 copy-done.1
  352.7 9.0 %convolution_bitcast_fusion = f32[1,2,1024,1024]{3,2,1,0:T(8,128)} fusion(bf16[2,1536,1024]{2,1,0:T(8,128)(2,1)S(1)} %copy-done.1, bf16[2,1536,1024]{2,1,0:T(8,128)(2,1)S(1)} %copy-done), kind=kOutput, calls=%fused_computation | convolution fusion | flops 6442450944 | bytes 20971520 | tf_op jit(solution)/shard_map/ktf,ktd->kfd/dot_general | solution.py:461
Async XLA Ops:
  339.9 12.8 %copy-start = (bf16[2,1536,1024]{2,1,0:T(8,128)(2,1)S(1)}, bf16[2,1536,1024]{2,1,0:T(8,128)(2,1)}, u32[]{:S(2)}) copy-start(bf16[2,1536,1024]{2,1,0:T(8,128)(2,1)} %get-tuple-element.11) | copy-start | bytes 18874372
  339.9 12.8 %copy-start.1 = (bf16[2,1536,1024]{2,1,0:T(8,128)(2,1)S(1)}, bf16[2,1536,1024]{2,1,0:T(8,128)(2,1)}, u32[]{:S(2)}) copy-start(bf16[2,1536,1024]{2,1,0:T(8,128)(2,1)} %get-tuple-element.10) | copy-start | bytes 18874372

commit v4 on v3

--- a/solution.py
+++ b/solution.py
@@ -92,7 +92,8 @@
         dc = lax.rem(dl // 2, 2)
         grad = last | jnp.logical_not(fwd)
         di = index_of(dl, m, j, dy) + jnp.where(grad, nd, 0)
-        return last, di, 2 * dy + dc, (dy == y) & (dc == core)
+        across = e["ext"] | (y1 & jnp.logical_not(fwd) & (l == 1))
+        return last, di, 2 * dy + dc, (dy == y) & (dc == core), across
 
     loads = []
     for k in range(2):
@@ -275,7 +276,7 @@
     def do_c(e):
         s, qr = lax.rem(e["n"], SR), q_slot(e)
         ai = index_of(e["l"], e["m"], e["j"], y) + jnp.where(e["fwd"], 0, nd)
-        last, di, ds, local = dest(e)
+        last, di, ds, local, across = dest(e)
         for c in range(NP):
             wait_in(qbuf.at[qr, c], qsem.at[qr, c])
             h = act[ai, c].astype(F32) + (sbuf[s, c].astype(F32) + qbuf[qr, c].astype(F32))
@@ -301,7 +302,7 @@
             def _():
                 rcopy(obuf.at[s, c], act.at[di, c], oosem.at[s], asem.at[di, c], z, ds).start()
 
-            @pl.when(jnp.logical_not(e["ext"]))
+            @pl.when(jnp.logical_not(across))
             def _():
                 rcopy(obuf.at[s, c], act.at[di, c], oesem.at[s], asem.at[di, c], partner, ds).start()
 
@@ -334,6 +335,10 @@
             for c in range(NP):
                 wait_in(act.at[nd + hi, c], asem.at[nd + hi, c])
 
+                @pl.when(is_mid)
+                def _():
+                    rcopy(act.at[nd + hi, c], act.at[nd + hi, c], pxsem, asem.at[nd + hi, c], partner, stage).start()
+
         put_act(nd + hi, k, m, d_out, outsem.at[1])
         up_bwd(hi, wi)
         put_hid(ubuf.at[hi], k, m, g_out, outsem.at[3])
@@ -352,8 +357,8 @@
         @pl.when(is_mid & eco["ar"])
         def _():
             s = lax.rem(n + SR - LC, SR)
-            pl.when(jnp.logical_not(eco["ext"]))(lambda: wait_in(obuf.at[s], oesem.at[s]))
-            local = dest(eco)[3]
+            local, across = dest(eco)[3:]
+            pl.when(jnp.logical_not(across))(lambda: wait_in(obuf.at[s], oesem.at[s]))
             pl.when(jnp.logical_not(local))(lambda: wait_in(obuf.at[s], oosem.at[s]))
 
         @pl.loop(relayed(n), relayed(n + 1))
@@ -408,7 +413,7 @@
     for full, sem in ((jnp.logical_not(y0 & c0), wssem), (jnp.logical_not(y1 & c0), wfsem)):
         pl.when(full)(functools.partial(wait_in, w.at[0], sem))
     pl.when(y1 & c0)(functools.partial(wait_in, w.at[0, 0], wfsem))
-    pl.when(y1 & c0 & is_mid)(functools.partial(wait_in, act.at[pl.ds(0, nh)], pxsem))
+    pl.when(c0 & is_mid)(functools.partial(wait_in, act.at[pl.ds(0, nh)], pxsem))
     half_ship = y1 & c0
     pl.when(half_ship)(functools.partial(wait_in, act.at[pl.ds(0, n_micro)], shsem))
     pl.when(jnp.logical_not(half_ship))(functools.partial(wait_in, act.at[pl.ds(0, 2 * n_micro)], shsem))

time: 362 us -> 372 us (1.028)
  Pallas kernels: 338 us -> 348 us
    pallas_call x1, Pallas kernels: 338 us -> 348 us  [device_program(): pl.pallas_call(functools.partial(step_kernel, n_micro, inv_count), out_sh...]
where the time goes in v4:
time: 372 us
  Pallas kernels  348 us (94%)
  matrix products  21.8 us (6%)
    pallas_call x1, Pallas kernels, device_program(): pl.pallas_call(functools.partial(step_kernel, n_micro, inv_count), out_sh...  348 us
    dot_general x1, matrix products, device_program(): jnp.einsum('ktd,ktf->kdf', a_s, g_s, preferred_element_type=F32)[None]  12.8 us
    dot_general x1, matrix products, device_program(): jnp.einsum('ktf,ktd->kfd', z_s, d_s, preferred_element_type=F32)[None]  8.99 us

profile of v4, /device:TPU:0, one launch (start us, length us, event | category | flops | bytes accessed | tf_op | source)
XLA Modules:
  0.0 371.8 jit_solution(2232876916207185570)
XLA Ops:
  0.6 348.1 %pipeline_step.1 = (bf16[2,1536,1024]{2,1,0:T(8,128)(2,1)}, bf16[2,1536,1024]{2,1,0:T(8,128)(2,1)}, bf16[2,1536,1024]{2,1,0:T(8,128)(2,1)}, bf16[2,1536,1024]{2,1,0:T(8,128)(2,1)}, f32[8,128]{1,0:T(8,128)}) custom-call(bf16[12,128,1024]{2,1,0:T(8,128)(2,1)} %x_hbm.1, bf16[12,128,1024]{2,1,0:T(8,128)(2,1)} %t_hbm.1, bf16[1,2,1024,1024]{3,2,1,0:T(8,128)(2,1)} %w1_hbm.1, ...), custom_call_target="tpu_custom_call" | custom-call | tf_op jit(solution)/shard_map/pipeline_step/pallas_call | solution.py:441
  348.8 1.2 slice.3
  350.0 0.0 copy-start
  350.0 0.0 copy-start.1
  350.0 12.8 %convolution_bitcast_fusion.1 = f32[1,2,1024,1024]{3,2,1,0:T(8,128)} fusion(bf16[2,1536,1024]{2,1,0:T(8,128)(2,1)} %get-tuple-element.8, bf16[2,1536,1024]{2,1,0:T(8,128)(2,1)} %get-tuple-element.9), kind=kOutput, calls=%fused_computation.1 | convolution fusion | flops 6442450944 | bytes 20971520 | tf_op jit(solution)/shard_map/ktd,ktf->kdf/dot_general | solution.py:465
  362.8 0.0 copy-done
  362.8 0.0 copy-done.1
  362.8 9.0 %convolution_bitcast_fusion = f32[1,2,1024,1024]{3,2,1,0:T(8,128)} fusion(bf16[2,1536,1024]{2,1,0:T(8,128)(2,1)S(1)} %copy-done.1, bf16[2,1536,1024]{2,1,0:T(8,128)(2,1)S(1)} %copy-done), kind=kOutput, calls=%fused_computation | convolution fusion | flops 6442450944 | bytes 20971520 | tf_op jit(solution)/shard_map/ktf,ktd->kfd/dot_general | solution.py:466
Async XLA Ops:
  350.0 12.8 %copy-start = (bf16[2,1536,1024]{2,1,0:T(8,128)(2,1)S(1)}, bf16[2,1536,1024]{2,1,0:T(8,128)(2,1)}, u32[]{:S(2)}) copy-start(bf16[2,1536,1024]{2,1,0:T(8,128)(2,1)} %get-tuple-element.11) | copy-start | bytes 18874372
  350.0 12.8 %copy-start.1 = (bf16[2,1536,1024]{2,1,0:T(8,128)(2,1)S(1)}, bf16[2,1536,1024]{2,1,0:T(8,128)(2,1)}, u32[]{:S(2)}) copy-start(bf16[2,1536,1024]{2,1,0:T(8,128)(2,1)} %get-tuple-element.10) | copy-start | bytes 18874372
